TPU v7x, 8 devices: a whole 2x2x1 slice. The times are simulated.
8 devices in a mesh: data: 1 (over z), cp: 2 (over y), tp: 4 (over x, core).
Axes of the slice: x: 2, y: 2, z: 1, core: 2. Of those that a mesh axis runs over, the one named last changes fastest.
Arguments:
- x_in: bfloat16 [4096, 2048], P(('data', 'cp', 'tp'))
- w_q: bfloat16 [2048, 32, 128], P(None, 'tp')
- w_k: bfloat16 [2048, 4, 128], P(None, 'tp')
- w_v: bfloat16 [2048, 4, 128], P(None, 'tp')
- w_o: bfloat16 [32, 128, 2048], P('tp')
- expert_idx: int32 [4096, 2], P(('data', 'cp', 'tp'))
- gate_wts: float32 [4096, 2], P(('data', 'cp', 'tp'))
- w_gate: bfloat16 [128, 2048, 768], P(('cp', 'tp'))
- w_up: bfloat16 [128, 2048, 768], P(('cp', 'tp'))
- w_down: bfloat16 [128, 768, 2048], P(('cp', 'tp'))
Outputs:
- output: bfloat16 [4096, 2048], P(('data', 'cp', 'tp'))
All inputs are finite; a program needn't handle non-finite values.
Results may differ from a plain program's by a relative error of at most 0.0146991.
Values are sent between devices in bfloat16 or wider.
A program may use at most 1 GiB of HBM per device.

v0:
```python
import jax
import jax.numpy as jnp
from jax import lax
from jax.sharding import PartitionSpec as P


def row_positions(cp_ranks, cp_size, tp_size, tok_dev):
    half_rows = tok_dev // 2
    local_rows = jnp.arange(tp_size * tok_dev)
    tp_src = local_rows // tok_dev
    within = local_rows % tok_dev
    seg_index = jnp.where((within < half_rows)[None, :], cp_ranks[:, None], 2 * cp_size - 1 - cp_ranks[:, None])
    offset = tp_src * half_rows + within % half_rows
    return (seg_index * (tp_size * half_rows) + offset[None, :]).reshape(-1)


def solution(mesh):
    cp_size = mesh.shape['cp']
    tp_size = mesh.shape['tp']
    num_devs = cp_size * tp_size
    row_spec = P(('data', 'cp', 'tp'), None)
    head_spec = P(None, 'tp', None)
    wo_spec = P('tp', None, None)
    expert_spec = P(('cp', 'tp'), None, None)

    def device_fn(x_blk, w_q, w_k, w_v, w_o, idx_blk, gate_blk, w_gate, w_up, w_down):
        tok_dev = x_blk.shape[0]
        kv_local, head_dim = w_k.shape[1], w_k.shape[2]
        q_per_kv = w_q.shape[1] // kv_local
        exp_local = w_gate.shape[0]
        num_exp = exp_local * num_devs
        capacity = 4 * tok_dev // num_exp
        cp_rank = lax.axis_index('cp')

        x_rows = lax.all_gather(x_blk, 'tp', axis=0, tiled=True)
        queries = jnp.einsum('sm,mnc->snc', x_rows, w_q, preferred_element_type=jnp.float32).astype(jnp.bfloat16)
        keys_loc = jnp.einsum('sm,mnc->snc', x_rows, w_k, preferred_element_type=jnp.float32).astype(jnp.bfloat16)
        vals_loc = jnp.einsum('sm,mnc->snc', x_rows, w_v, preferred_element_type=jnp.float32).astype(jnp.bfloat16)
        keys_all = lax.all_gather(keys_loc, 'cp', axis=0, tiled=True)
        vals_all = lax.all_gather(vals_loc, 'cp', axis=0, tiled=True)
        pos_q = row_positions(cp_rank.reshape(1), cp_size, tp_size, tok_dev)
        pos_k = row_positions(jnp.arange(cp_size), cp_size, tp_size, tok_dev)
        q_grp = queries.reshape(-1, kv_local, q_per_kv, head_dim)
        scores = jnp.einsum('qngc,knc->ngqk', q_grp, keys_all, preferred_element_type=jnp.float32) * (head_dim ** -0.5)
        scores = jnp.where(pos_k[None, None, None, :] <= pos_q[None, None, :, None], scores, -jnp.inf)
        exp_scores = jnp.exp(scores - jnp.max(scores, axis=-1, keepdims=True))
        attn_prob = (exp_scores / jnp.sum(exp_scores, axis=-1, keepdims=True)).astype(jnp.bfloat16)
        head_out = jnp.einsum('ngqk,knc->qngc', attn_prob, vals_all, preferred_element_type=jnp.float32).astype(jnp.bfloat16)
        part_sum = jnp.einsum('qngc,ngcm->qm', head_out, w_o.reshape(kv_local, q_per_kv, head_dim, -1), preferred_element_type=jnp.float32)
        attn_out = lax.psum_scatter(part_sum, 'tp', scatter_dimension=0, tiled=True)
        hidden = (x_blk.astype(jnp.float32) + attn_out).astype(jnp.bfloat16)

        flat_ids = idx_blk.reshape(-1)
        onehot = (flat_ids[:, None] == jnp.arange(num_exp)[None, :]).astype(jnp.int32)
        slot_pos = jnp.sum(jnp.cumsum(onehot, axis=0) * onehot, axis=1) - 1
        slot_ids = (flat_ids * capacity + slot_pos).reshape(tok_dev, 2)
        select = (slot_ids[:, :, None] == jnp.arange(num_exp * capacity)[None, None, :]).astype(jnp.bfloat16)
        send_buf = jnp.einsum('tkn,tm->nm', select, hidden, preferred_element_type=jnp.float32).astype(jnp.bfloat16)
        recv_buf = lax.all_to_all(send_buf, ('cp', 'tp'), 0, 0, tiled=True)
        tok_in = recv_buf.reshape(num_devs, exp_local, capacity, -1)
        gate_pre = jnp.einsum('secm,emf->secf', tok_in, w_gate, preferred_element_type=jnp.float32)
        up_pre = jnp.einsum('secm,emf->secf', tok_in, w_up, preferred_element_type=jnp.float32)
        hid_act = (jax.nn.silu(gate_pre) * up_pre).astype(jnp.bfloat16)
        exp_out = jnp.einsum('secf,efm->secm', hid_act, w_down, preferred_element_type=jnp.float32).astype(jnp.bfloat16)
        back_buf = lax.all_to_all(exp_out.reshape(num_devs * exp_local * capacity, -1), ('cp', 'tp'), 0, 0, tiled=True)
        picked = jnp.einsum('tkn,nm->tkm', select, back_buf, preferred_element_type=jnp.float32)
        moe_out = jnp.sum(gate_blk[:, :, None] * picked, axis=1)
        return (hidden.astype(jnp.float32) + moe_out).astype(jnp.bfloat16)

    return jax.shard_map(device_fn, mesh=mesh, in_specs=(row_spec, head_spec, head_spec, head_spec, wo_spec, row_spec, row_spec, expert_spec, expert_spec, expert_spec), out_specs=row_spec, check_vma=False)
```

profile of v0, /device:TPU:0, one launch (start us, length us, event | category | flops | bytes accessed | tf_op | source)
XLA Modules:
  0.0 795.8 jit_solution(2911189983008590336)
XLA Ops:
  6.5 0.0 all-gather.6.cloned.1.call-start
  6.5 0.7 all-gather.6.cloned.1.call-update
  7.3 0.0 all-gather.10.cloned.1.call-start
  7.3 0.1 add_bitcast_fusion
  7.5 0.0 copy-start.8
  7.5 60.0 %all-gather.6.cloned.1.call-done = bf16[2048,2048]{1,0:T(8,128)(2,1)} async-done(((bf16[512,2048]{1,0:T(8,128)(2,1)}), bf16[2048,2048]{1,0:T(8,128)(2,1)}) %all-gather.6.cloned.1.call-update) | async-done | bytes 8388624 | tf_op jit(solution)/shard_map/all_gather | solution.py:35
  67.4 6.5 convolution_convert_fusion.1
  74.0 0.0 all-gather.10.cloned.1.call-update
  74.0 0.0 all-gather.8.cloned.1.call-start
  74.1 7.6 broadcast_compare_fusion
  81.7 0.0 copy-done.6
  81.7 3.2 convolution_convert_fusion.2
  84.9 0.0 all-gather.8.cloned.1.call-update
  84.9 0.3 reduce-scatter.2.cloned.1.call-start
  85.3 13.8 %fusion.10 = bf16[2048,8,128]{2,0,1:T(8,128)(2,1)} fusion(bf16[2048,2048]{1,0:T(8,128)(2,1)} %all-gather.6.cloned.1.call-done, bf16[2048,8,128]{2,1,0:T(8,128)(2,1)} %param.11), kind=kOutput, calls=%fused_computation.15 | convolution fusion | flops 8589934592 | bytes 16777216 | tf_op jit(solution)/shard_map/sm,mnc->snc/dot_general | solution.py:36
  99.1 90.7 %fusion.1 = (f32[8,2048]{1,0:T(8,128)S(1)}, f32[4096,2048,8]{1,0,2:T(8,128)}) fusion(pred[2048,4096]{0,1:T(8,128)(4,1)} %broadcast_compare_fusion, bf16[2048,8,128]{2,0,1:T(8,128)(2,1)} %fusion.10, bf16[4096,128]{1,0:T(8,128)(2,1)} %all-gather.10.cloned.1.call-done), kind=kOutput, calls=%fused_computation.4 | convolution fusion | flops 17381179392 | bytes 282132480 | tf_op jit(solution)/shard_map/qngc,knc->ngqk/dot_general | solution.py:44
  189.8 83.2 %fusion = f32[8,2048]{1,0:T(8,128)S(1)} fusion(f32[4096,2048,8]{1,0,2:T(8,128)} %get-tuple-element.6, f32[8,2048]{1,0:T(8,128)S(1)} %get-tuple-element.5, pred[2048,4096]{0,1:T(8,128)(4,1)} %broadcast_compare_fusion), kind=kLoop, calls=%fused_computation.3 | loop fusion | flops 268419072 | bytes 276955136 | tf_op jit(solution)/shard_map/reduce_sum | solution.py:47
  273.0 0.0 all-gather.8.cloned.1.call-done
  273.0 0.0 copy-start.7
  273.0 90.7 %fusion.2 = bf16[128,8,2048]{2,0,1:T(8,128)(2,1)S(1)} fusion(f32[4096,2048,8]{1,0,2:T(8,128)} %get-tuple-element.6, f32[8,2048]{1,0:T(8,128)S(1)} %fusion, f32[8,2048]{1,0:T(8,128)S(1)} %get-tuple-element.5, pred[2048,4096]{0,1:T(8,128)(4,1)} %broadcast_compare_fusion, bf16[4096,128]{1,0:T(8,128)(2,1)} %all-gather.8.cloned.1.call-done), kind=kOutput, calls=%fused_computation.5 | convolution fusion | flops 17515413504 | bytes 282198016 | tf_op jit(solution)/shard_map/ngqk,knc->qngc/dot_general | solution.py:48
  363.7 0.0 copy-done.7
  363.7 11.9 %convolution_bitcast_fusion = f32[2048,2048]{1,0:T(8,128)} fusion(bf16[8,128,2048]{2,1,0:T(8,128)(2,1)S(1)} %copy-done.7, bf16[128,8,2048]{2,0,1:T(8,128)(2,1)S(1)} %fusion.2), kind=kOutput, calls=%fused_computation.14 | convolution fusion | flops 8589934592 | bytes 25165824 | tf_op jit(solution)/shard_map/qngc,ngcm->qm/dot_general | solution.py:49
  375.6 0.0 copy-start.5
  375.6 0.0 copy-start.3
  375.6 0.0 reduce-scatter.2.cloned.1.call-update
  375.6 0.6 copy-done.5
  376.3 0.1 copy.28
  376.4 0.2 eq.47
  376.6 0.2 eq.43
  376.8 0.1 copy.30
  376.9 0.2 fusion.42
  377.2 0.1 copy.31
  377.3 0.4 fusion.39
  377.7 0.2 sub.42
  377.9 0.1 copy.32
  378.0 2.4 convert_reduce_fusion
  380.3 114.2 %reduce-scatter.2.cloned.1.call-done = f32[512,2048]{1,0:T(8,128)} async-done(((f32[2048,2048]{1,0:T(8,128)}), f32[512,2048]{1,0:T(8,128)}) %reduce-scatter.2.cloned.1.call-update) | async-done | bytes 4194320 | tf_op jit(solution)/shard_map/reduce_scatter | solution.py:50
  494.5 10.6 %convolution_convert_fusion = bf16[2048,2048]{1,0:T(8,128)(2,1)} fusion(bf16[512,2048]{1,0:T(8,128)(2,1)} %convert_reduce_fusion, f32[512,2048]{1,0:T(8,128)} %reduce-scatter.2.cloned.1.call-done, bf16[512,2048]{1,0:T(8,128)(2,1)S(1)} %copy-done.3), kind=kOutput, calls=%fused_computation.23 | convolution fusion | flops 4298113024 | bytes 16777216 | tf_op jit(solution)/shard_map/tkn,tm->nm/dot_general | solution.py:58
  505.1 96.5 %all_to_all.21 = bf16[8,256,2048]{2,1,0:T(8,128)(2,1)S(1)} all-to-all(bf16[8,256,2048]{2,1,0:T(8,128)(2,1)} %bitcast.121), channel_id=1, replica_groups=mesh['data'=1,'cp'=2,'tp'=4] {'cp','tp'}, dimensions={0} | all-to-all | bytes 16777216 | tf_op jit(solution)/shard_map/all_to_all | solution.py:59
  601.7 3.2 copy-done.2
  604.9 20.3 %fusion.6 = f32[16,8,16,768]{3,2,1,0:T(8,128)} fusion(bf16[16,2048,768]{2,1,0:T(8,128)(2,1)} %param.18, bf16[8,16,16,2048]{3,2,1,0:T(8,128)(2,1)S(1)} %bitcast.118), kind=kOutput, calls=%fused_computation.9 | convolution fusion | flops 6442450944 | bytes 65011712 | tf_op jit(solution)/shard_map/secm,emf->secf/dot_general | solution.py:62
  625.2 47.1 %convert_bitcast_fusion = bf16[8,16,16,2048]{3,2,0,1:T(8,128)(2,1)} fusion(bf16[16,768,2048]{2,1,0:T(8,128)(2,1)} %param.19, f32[16,8,16,768]{3,2,1,0:T(8,128)} %fusion.6, bf16[16,2048,768]{2,1,0:T(8,128)(2,1)} %param.17, bf16[8,16,16,2048]{3,2,1,0:T(8,128)(2,1)} %bitcast.119), kind=kOutput, calls=%fused_computation.18 | convolution fusion | flops 12898533376 | bytes 123731968 | tf_op jit(solution)/shard_map/secf,efm->secm/dot_general | solution.py:64
  672.3 8.3 %copy.35 = bf16[8,16,16,2048]{3,2,1,0:T(8,128)(2,1)} copy(bf16[8,16,16,2048]{3,2,0,1:T(8,128)(2,1)} %convert_bitcast_fusion) | data formatting | bytes 16777216 | tf_op jit(solution)/shard_map/convert_element_type | solution.py:64
  680.6 96.5 %all_to_all.22 = bf16[8,256,2048]{2,1,0:T(8,128)(2,1)S(1)} all-to-all(bf16[8,256,2048]{2,1,0:T(8,128)(2,1)} %bitcast.117), channel_id=1, replica_groups=mesh['data'=1,'cp'=2,'tp'=4] {'cp','tp'}, dimensions={0} | all-to-all | bytes 16777216 | tf_op jit(solution)/shard_map/all_to_all | solution.py:65
  777.0 0.0 copy-done.9
  777.0 9.4 %multiply_reduce_fusion = f32[512,2048]{1,0:T(8,128)S(1)} fusion(f32[512,2]{0,1:T(2,128)S(1)} %copy-done.9, bf16[2048,2048,1]{1,0,2:T(8,128)(2,1)S(1)} %bitcast.120, s32[512,2]{0,1:T(2,128)S(1)} %multiply_add_fusion.1), kind=kOutput, calls=%fused_computation.17 | convolution fusion | flops 8595177472 | bytes 12591104 | tf_op jit(solution)/shard_map/tkn,nm->tkm/dot_general | solution.py:66
  786.5 0.0 copy-done.4
  786.5 2.5 add_convert_fusion
  (22 shorter events, 0.1 us)
Async XLA Ops:
  6.5 60.9 %copy-start = (bf16[2048,1,128]{2,0,1:T(8,128)(2,1)S(1)}, bf16[2048,1,128]{2,0,1:T(8,128)(2,1)}, u32[]{:S(2)}) copy-start(bf16[2048,1,128]{2,0,1:T(8,128)(2,1)} %param.12) | copy-start | bytes 1572868
  6.5 60.9 %all-gather.6.cloned.1.call-start = ((), (), s32[]{:S(2)}) async-start(), calls=%async_computation.3 | async-start | bytes 10485760 | tf_op jit(solution)/shard_map/all_gather | solution.py:35
  7.3 91.8 %all-gather.10.cloned.1.call-start = ((), (), s32[]{:S(2)}) async-start(), calls=%async_computation.6 | async-start | bytes 1572864 | tf_op jit(solution)/shard_map/all_gather | solution.py:39
  7.5 74.2 %copy-start.8 = (bf16[2048,1,128]{2,0,1:T(8,128)(2,1)S(1)}, bf16[2048,1,128]{2,0,1:T(8,128)(2,1)}, u32[]{:S(2)}) copy-start(bf16[2048,1,128]{2,0,1:T(8,128)(2,1)} %param.13) | copy-start | bytes 1572868
  74.0 199.0 %all-gather.8.cloned.1.call-start = ((), (), s32[]{:S(2)}) async-start(), calls=%async_computation.5 | async-start | bytes 1572864 | tf_op jit(solution)/shard_map/all_gather | solution.py:40
  74.0 7.6 copy-start.6
  84.9 409.6 %reduce-scatter.2.cloned.1.call-start = ((), (), s32[]{:S(2)}) async-start(), calls=%async_computation.4 | async-start | bytes 20971520 | tf_op jit(solution)/shard_map/reduce_scatter | solution.py:50
  273.0 90.7 %copy-start.7 = (bf16[8,128,2048]{2,1,0:T(8,128)(2,1)S(1)}, bf16[8,128,2048]{2,1,0:T(8,128)(2,1)}, u32[]{:S(2)}) copy-start(bf16[8,128,2048]{2,1,0:T(8,128)(2,1)} %param.14) | copy-start | bytes 12582916
  375.6 0.7 copy-start.5
  375.6 118.9 %copy-start.3 = (bf16[512,2048]{1,0:T(8,128)(2,1)S(1)}, bf16[512,2048]{1,0:T(8,128)(2,1)}, u32[]{:S(2)}) copy-start(bf16[512,2048]{1,0:T(8,128)(2,1)} %param.10) | copy-start | bytes 6291460
  601.7 3.2 copy-start.2
  680.6 96.5 %copy-start.9 = (f32[512,2]{0,1:T(2,128)S(1)}, f32[512,2]{0,1:T(2,128)}, u32[]{:S(2)}) copy-start(f32[512,2]{0,1:T(2,128)} %param.16) | copy-start | bytes 12292
  777.0 9.5 %copy-start.4 = (f32[512,2048]{1,0:T(8,128)S(1)}, f32[512,2048]{1,0:T(8,128)}, u32[]{:S(2)}) copy-start(f32[512,2048]{1,0:T(8,128)} %reduce-scatter.2.cloned.1.call-done) | copy-start | bytes 12582916
  777.0 12.0 %copy-start.1 = (bf16[2048,1,128]{2,0,1:T(8,128)(2,1)S(1)}, bf16[2048,1,128]{2,0,1:T(8,128)(2,1)}, u32[]{:S(2)}) copy-start(bf16[2048,1,128]{2,0,1:T(8,128)(2,1)} %param.12) | copy-start | bytes 1572868
Sparse Core Ops, SparseCore 0:
  8.9 58.5 all-gather.5
  74.1 18.2 all-gather.9
  93.9 18.2 all-gather.7
  375.8 118.7 reduce-scatter.1
where the time goes:
time: 800 us; the launch traced here: 796 us
  matrix products  304 us (38%)
  blocking collectives  193 us (24%)
  waiting for transfers between devices  175 us (22%)
  other arithmetic  96.4 us (12%)
  between operations  13.6 us (2%)
  local copies, waits for them, and re-layouts  13.1 us (2%)
    reduce_scatter x1, waiting for transfers between devices, device_fn(): attn_out = lax.psum_scatter(part_sum, 'tp', scatter_dimension=0, tiled=True)  114 us
    all_to_all x1, blocking collectives, device_fn(): recv_buf = lax.all_to_all(send_buf, ('cp', 'tp'), 0, 0, tiled=True)  96.5 us
    all_to_all x1, blocking collectives, device_fn(): lax.all_to_all(exp_out.reshape(num_devs * exp_local * capacity, -1), ('cp...  96.5 us
    dot_general x1, matrix products, device_fn(): jnp.einsum('qngc,knc->ngqk', q_grp, keys_all, preferred_element_type=jnp....  90.7 us
    dot_general x1, matrix products, device_fn(): jnp.einsum('ngqk,knc->qngc', attn_prob, vals_all, preferred_element_type=...  90.7 us
    reduce_sum x1, other arithmetic, device_fn(): jnp.sum(exp_scores, axis=-1, keepdims=True)  83.2 us
    all_gather x1, waiting for transfers between devices, device_fn(): x_rows = lax.all_gather(x_blk, 'tp', axis=0, tiled=True)  60 us
    dot_general x1, matrix products, device_fn(): jnp.einsum('secf,efm->secm', hid_act, w_down, preferred_element_type=jnp....  47.1 us
  transfers between devices with their start and end apart: 4, of which 2 were waited for; matrix products, arithmetic and copies ran while one was open for 25% of the time, Pallas kernels for 0%

commit v1 on v0

v1 whole, which is shorter than its diff:
```python
import functools
import jax
import jax.numpy as jnp
from jax import lax
from jax.experimental import pallas as pl
from jax.experimental.pallas import tpu as pltpu
from jax.sharding import PartitionSpec as P

QB = 256
KB = 512
LOG2E = 1.4426950408889634
VLIM = 62 * 1024 * 1024


def attend_block(q_of, k_ref, v_ref, m_ref, l_ref, acc_ref, pos0, heads, hd):
    c = (hd ** -0.5) * LOG2E
    m_ref[...] = jnp.full(m_ref.shape, -jnp.inf, jnp.float32)
    l_ref[...] = jnp.zeros(l_ref.shape, jnp.float32)
    acc_ref[...] = jnp.zeros(acc_ref.shape, jnp.float32)

    def step(kb, masked):
        start = pl.multiple_of(kb * KB, KB)
        k = k_ref[pl.ds(start, KB), :]
        v = v_ref[pl.ds(start, KB), :]
        for h in range(heads):
            rows = slice(h * QB, (h + 1) * QB)
            s = lax.dot_general(q_of(h), k, (((1,), (1,)), ((), ())), preferred_element_type=jnp.float32)
            if masked:
                qp = pos0 + lax.broadcasted_iota(jnp.int32, (QB, KB), 0)
                kp = start + lax.broadcasted_iota(jnp.int32, (QB, KB), 1)
                s = jnp.where(kp <= qp, s, -jnp.inf)
            m_old = m_ref[rows, :]
            m_new = jnp.maximum(m_old, jnp.max(s, axis=1, keepdims=True))
            alpha = jnp.exp2((m_old - m_new) * c)
            p = jnp.exp2((s - jnp.concatenate([m_new] * (KB // 128), axis=1)) * c)
            lp = p[:, :128]
            for j in range(1, KB // 128):
                lp = lp + p[:, j * 128:(j + 1) * 128]
            m_ref[rows, :] = m_new
            l_ref[rows, :] = l_ref[rows, :] * alpha + lp
            acc_ref[rows, :] = acc_ref[rows, :] * alpha + jnp.dot(p.astype(jnp.bfloat16), v, preferred_element_type=jnp.float32)

    last = pos0 // KB

    def body(kb, carry):
        step(kb, False)
        return carry

    lax.fori_loop(0, last, body, 0)
    step(last, True)


def attn_kernel(cp_size, tp_size, heads, hd, q_ref, k_ref, v_ref, wo_ref, o_ref, m_ref, l_ref, acc_ref, ob_ref):
    b = pl.program_id(0)
    r = lax.axis_index('cp')
    t_src = b // 2
    half = b % 2
    seg = r + half * (2 * cp_size - 1 - 2 * r)
    pos0 = (seg * tp_size + t_src) * QB
    attend_block(lambda h: q_ref[:, h * hd:(h + 1) * hd], k_ref, v_ref, m_ref, l_ref, acc_ref, pos0, heads, hd)
    for h in range(heads):
        rows = slice(h * QB, (h + 1) * QB)
        den = jnp.sum(l_ref[rows, :], axis=1, keepdims=True)
        ob_ref[:, h * hd:(h + 1) * hd] = (acc_ref[rows, :] / den).astype(jnp.bfloat16)
    o_ref[...] = jnp.dot(ob_ref[...], wo_ref[...], preferred_element_type=jnp.float32)


def solution(mesh):
    cp_size = mesh.shape['cp']
    tp_size = mesh.shape['tp']
    num_devs = cp_size * tp_size
    row_spec = P(('data', 'cp', 'tp'), None)
    head_spec = P(None, 'tp', None)
    wo_spec = P('tp', None, None)
    expert_spec = P(('cp', 'tp'), None, None)

    def attention(queries, keys, vals, w_o, heads, hd):
        rows, width = queries.shape[0], w_o.shape[1]
        seq = keys.shape[0]
        full = lambda shape: pl.BlockSpec(shape, lambda b: (0, 0))
        return pl.pallas_call(
            functools.partial(attn_kernel, cp_size, tp_size, heads, hd),
            grid=(rows // QB,),
            in_specs=[pl.BlockSpec((QB, heads * hd), lambda b: (b, 0)), full((seq, hd)), full((seq, hd)), full((heads * hd, width))],
            out_specs=pl.BlockSpec((QB, width), lambda b: (b, 0)),
            out_shape=jax.ShapeDtypeStruct((rows, width), jnp.float32),
            scratch_shapes=[pltpu.VMEM((heads * QB, 128), jnp.float32), pltpu.VMEM((heads * QB, 128), jnp.float32), pltpu.VMEM((heads * QB, hd), jnp.float32), pltpu.VMEM((QB, heads * hd), jnp.bfloat16)],
            name='attn',
        )(queries, keys, vals, w_o)

    def device_fn(x_blk, w_q, w_k, w_v, w_o, idx_blk, gate_blk, w_gate, w_up, w_down):
        tok_dev, width = x_blk.shape
        heads, head_dim = w_q.shape[1], w_k.shape[2]
        exp_local = w_gate.shape[0]
        num_exp = exp_local * num_devs
        capacity = 4 * tok_dev // num_exp

        x_rows = lax.all_gather(x_blk, 'tp', axis=0, tiled=True)
        mm = lambda a, w: jnp.dot(a, w.reshape(width, -1), preferred_element_type=jnp.float32).astype(jnp.bfloat16)
        queries = mm(x_rows, w_q)
        kv_loc = jnp.stack([mm(x_rows, w_k), mm(x_rows, w_v)])
        kv_all = lax.all_gather(kv_loc, 'cp', axis=0)
        kv_all = kv_all.reshape(cp_size, 2, tp_size, 2, QB, head_dim)
        order = [kv_all[s, :, :, 0] for s in range(cp_size)] + [kv_all[cp_size - 1 - s, :, :, 1] for s in range(cp_size)]
        kv_pos = jnp.stack(order, axis=1).reshape(2, -1, head_dim)
        part_sum = attention(queries, kv_pos[0], kv_pos[1], w_o.reshape(heads * head_dim, width), heads, head_dim)
        attn_out = lax.psum_scatter(part_sum, 'tp', scatter_dimension=0, tiled=True)
        hidden = (x_blk.astype(jnp.float32) + attn_out).astype(jnp.bfloat16)

        flat_ids = idx_blk.reshape(-1)
        onehot = (flat_ids[:, None] == jnp.arange(num_exp)[None, :]).astype(jnp.int32)
        slot_pos = jnp.sum(jnp.cumsum(onehot, axis=0) * onehot, axis=1) - 1
        slot_ids = (flat_ids * capacity + slot_pos).reshape(tok_dev, 2)
        select = (slot_ids[:, :, None] == jnp.arange(num_exp * capacity)[None, None, :]).astype(jnp.bfloat16)
        send_buf = jnp.einsum('tkn,tm->nm', select, hidden, preferred_element_type=jnp.float32).astype(jnp.bfloat16)
        recv_buf = lax.all_to_all(send_buf, ('cp', 'tp'), 0, 0, tiled=True)
        tok_in = recv_buf.reshape(num_devs, exp_local, capacity, -1)
        gate_pre = jnp.einsum('secm,emf->secf', tok_in, w_gate, preferred_element_type=jnp.float32)
        up_pre = jnp.einsum('secm,emf->secf', tok_in, w_up, preferred_element_type=jnp.float32)
        hid_act = (jax.nn.silu(gate_pre) * up_pre).astype(jnp.bfloat16)
        exp_out = jnp.einsum('secf,efm->secm', hid_act, w_down, preferred_element_type=jnp.float32).astype(jnp.bfloat16)
        back_buf = lax.all_to_all(exp_out.reshape(num_devs * exp_local * capacity, -1), ('cp', 'tp'), 0, 0, tiled=True)
        picked = jnp.einsum('tkn,nm->tkm', select, back_buf, preferred_element_type=jnp.float32)
        moe_out = jnp.sum(gate_blk[:, :, None] * picked, axis=1)
        return (hidden.astype(jnp.float32) + moe_out).astype(jnp.bfloat16)

    return jax.shard_map(device_fn, mesh=mesh, in_specs=(row_spec, head_spec, head_spec, head_spec, wo_spec, row_spec, row_spec, expert_spec, expert_spec, expert_spec), out_specs=row_spec, check_vma=False)
```

time: 800 us -> 642 us (0.80)
  matrix products: 304 us -> 110 us
  Pallas kernels: 0 us -> 111 us
  other arithmetic: 96.4 us -> 6.83 us
  waiting for transfers between devices: 175 us -> 191 us
    dot_general x6 -> x3, matrix products: 217 us -> 22 us  [device_fn(): jnp.dot(a, w.reshape(width, -1), preferred_element_type=jnp.float32)]
    pallas_call x0 -> x1, Pallas kernels: none -> 111 us  [attention(): pl.pallas_call(functools.partial(attn_kernel, cp_size, tp_size, heads, hd...]
    reduce_sum x1 -> x0, other arithmetic: 83.2 us -> none  [device_fn(): jnp.sum(exp_scores, axis=-1, keepdims=True)]
    all_gather x2 -> x1, waiting for transfers between devices: 0.02 us -> 16.3 us  [device_fn(): kv_all = lax.all_gather(kv_loc, 'cp', axis=0)]
  transfers between devices with their start and end apart: 4 -> 3, of which waited for: 2 -> 3; matrix products, arithmetic and copies ran while one was open for 25% -> 3% of each run, Pallas kernels for 0% -> 0%
where the time goes in v1:
time: 642 us; the launch traced here: 641 us
  blocking collectives  193 us (30%)
  waiting for transfers between devices  191 us (30%)
  Pallas kernels  111 us (17%)
  matrix products  110 us (17%)
  local copies, waits for them, and re-layouts  16.3 us (3%)
  between operations  13.2 us (2%)
  other arithmetic  6.83 us (1%)
    reduce_scatter x1, waiting for transfers between devices, device_fn(): attn_out = lax.psum_scatter(part_sum, 'tp', scatter_dimension=0, tiled=True)  114 us
    pallas_call x1, Pallas kernels, attention(): pl.pallas_call(functools.partial(attn_kernel, cp_size, tp_size, heads, hd...  111 us
    all_to_all x1, blocking collectives, device_fn(): lax.all_to_all(exp_out.reshape(num_devs * exp_local * capacity, -1), ('cp...  96.5 us
    all_to_all x1, blocking collectives, device_fn(): recv_buf = lax.all_to_all(send_buf, ('cp', 'tp'), 0, 0, tiled=True)  96.3 us
    all_gather x1, waiting for transfers between devices, device_fn(): x_rows = lax.all_gather(x_blk, 'tp', axis=0, tiled=True)  60.1 us
    dot_general x1, matrix products, device_fn(): jnp.einsum('secf,efm->secm', hid_act, w_down, preferred_element_type=jnp....  47.2 us
    dot_general x3, matrix products, device_fn(): jnp.dot(a, w.reshape(width, -1), preferred_element_type=jnp.float32)  22 us
    dot_general x1, matrix products, device_fn(): jnp.einsum('secm,emf->secf', tok_in, w_up, preferred_element_type=jnp.flo...  20.3 us
  transfers between devices with their start and end apart: 3, of which 3 were waited for; matrix products, arithmetic and copies ran while one was open for 3% of the time, Pallas kernels for 0%

profile of v1, /device:TPU:0, one launch (start us, length us, event | category | flops | bytes accessed | tf_op | source)
XLA Modules:
  0.0 641.5 jit_solution(14535169413028938724)
XLA Ops:
  6.5 0.0 copy-start
  6.5 0.0 all-gather.4.cloned.1.call-start
  6.5 0.7 all-gather.4.cloned.1.call-update
  7.3 0.0 copy-start.7
  7.3 0.0 all-gather.6.cloned.1.call-start
  7.3 60.1 %all-gather.4.cloned.1.call-done = bf16[2048,2048]{1,0:T(8,128)(2,1)} async-done(((bf16[512,2048]{1,0:T(8,128)(2,1)}), bf16[2048,2048]{1,0:T(8,128)(2,1)}) %all-gather.4.cloned.1.call-update) | async-done | bytes 8388624 | tf_op jit(solution)/shard_map/all_gather | solution.py:98
  67.4 0.0 copy-done
  67.5 5.9 fusion.33
  73.3 0.0 copy-done.7
  73.3 0.0 copy-done.6
  73.3 2.4 fusion.32
  75.8 1.1 pad_maximum_fusion.1
  76.8 0.0 all-gather.6.cloned.1.call-update
  76.8 0.2 reduce-scatter.2.cloned.1.call-start
  77.1 13.8 %fusion.28.q_ref = bf16[2048,1024]{1,0:T(8,128)(2,1)} fusion(bf16[2048,2048]{1,0:T(8,128)(2,1)} %all-gather.4.cloned.1.call-done, bf16[256,8,8,128]{3,2,1,0:T(8,128)(2,1)} %bitcast.116), kind=kOutput, calls=%fused_computation.28 | convolution fusion | flops 8592031744 | bytes 16777216 | tf_op jit(solution)/shard_map/dot_general | solution.py:99
  90.8 16.3 %all-gather.6.cloned.1.call-done = bf16[4,2048,128]{2,1,0:T(8,128)(2,1)} async-done(((bf16[2,2048,128]{2,1,0:T(8,128)(2,1)}), bf16[4,2048,128]{2,1,0:T(8,128)(2,1)}) %all-gather.6.cloned.1.call-update) | async-done | bytes 2097168 | tf_op jit(solution)/shard_map/all_gather | solution.py:102
  107.1 1.7 slice_bitcast_fusion.3
  108.8 0.3 pad_maximum_fusion
  109.1 1.5 fusion.41
  110.6 111.2 %attn.1 = f32[2048,2048]{1,0:T(8,128)} custom-call(bf16[2048,1024]{1,0:T(8,128)(2,1)} %fusion.28.q_ref, bf16[4096,128]{1,0:T(8,128)(2,1)} %bitcast.114, bf16[4096,128]{1,0:T(8,128)(2,1)} %bitcast.113, bf16[1024,2048]{1,0:T(8,128)(2,1)} %bitcast.112), custom_call_target="tpu_custom_call" | custom-call | tf_op jit(solution)/shard_map/attn/pallas_call | solution.py:81
  221.7 0.0 copy-start.5
  221.7 0.0 reduce-scatter.2.cloned.1.call-update
  221.8 0.7 copy-done.5
  222.4 0.0 copy-start.3
  222.4 0.1 copy.46
  222.6 0.2 eq.42
  222.7 0.2 eq.38
  222.9 0.1 copy.48
  223.0 0.2 fusion.37
  223.3 0.1 copy.49
  223.4 0.4 fusion.34
  223.8 0.2 sub.7
  224.0 0.1 copy.50
  224.1 2.4 convert_reduce_fusion
  226.5 114.2 %reduce-scatter.2.cloned.1.call-done = f32[512,2048]{1,0:T(8,128)} async-done(((f32[2048,2048]{1,0:T(8,128)}), f32[512,2048]{1,0:T(8,128)}) %reduce-scatter.2.cloned.1.call-update) | async-done | bytes 4194320 | tf_op jit(solution)/shard_map/reduce_scatter | solution.py:107
  340.7 0.0 copy-done.3
  340.7 10.6 %convolution_convert_fusion = bf16[2048,2048]{1,0:T(8,128)(2,1)} fusion(bf16[512,2048]{1,0:T(8,128)(2,1)} %convert_reduce_fusion, f32[512,2048]{1,0:T(8,128)} %reduce-scatter.2.cloned.1.call-done, bf16[512,2048]{1,0:T(8,128)(2,1)S(1)} %copy-done.3), kind=kOutput, calls=%fused_computation.12 | convolution fusion | flops 4298113024 | bytes 16777216 | tf_op jit(solution)/shard_map/tkn,tm->nm/dot_general | solution.py:115
  351.3 96.3 %all_to_all.21 = bf16[8,256,2048]{2,1,0:T(8,128)(2,1)S(1)} all-to-all(bf16[8,256,2048]{2,1,0:T(8,128)(2,1)} %bitcast.111), channel_id=1, replica_groups=mesh['data'=1,'cp'=2,'tp'=4] {'cp','tp'}, dimensions={0} | all-to-all | bytes 16777216 | tf_op jit(solution)/shard_map/all_to_all | solution.py:116
  447.6 3.2 copy-done.2
  450.8 20.3 %fusion.2 = f32[16,8,16,768]{3,2,1,0:T(8,128)} fusion(bf16[16,2048,768]{2,1,0:T(8,128)(2,1)} %param.18, bf16[8,16,16,2048]{3,2,1,0:T(8,128)(2,1)S(1)} %bitcast.108), kind=kOutput, calls=%fused_computation.2 | convolution fusion | flops 6442450944 | bytes 65011712 | tf_op jit(solution)/shard_map/secm,emf->secf/dot_general | solution.py:119
  471.1 47.2 %convert_bitcast_fusion = bf16[8,16,16,2048]{3,2,0,1:T(8,128)(2,1)} fusion(bf16[16,768,2048]{2,1,0:T(8,128)(2,1)} %param.19, f32[16,8,16,768]{3,2,1,0:T(8,128)} %fusion.2, bf16[16,2048,768]{2,1,0:T(8,128)(2,1)} %param.17, bf16[8,16,16,2048]{3,2,1,0:T(8,128)(2,1)} %bitcast.109), kind=kOutput, calls=%fused_computation.7 | convolution fusion | flops 12898533376 | bytes 123731968 | tf_op jit(solution)/shard_map/secf,efm->secm/dot_general | solution.py:121
  518.2 8.3 %copy.53 = bf16[8,16,16,2048]{3,2,1,0:T(8,128)(2,1)} copy(bf16[8,16,16,2048]{3,2,0,1:T(8,128)(2,1)} %convert_bitcast_fusion) | data formatting | bytes 16777216 | tf_op jit(solution)/shard_map/convert_element_type | solution.py:121
  526.5 96.5 %all_to_all.22 = bf16[8,256,2048]{2,1,0:T(8,128)(2,1)S(1)} all-to-all(bf16[8,256,2048]{2,1,0:T(8,128)(2,1)} %bitcast.107), channel_id=1, replica_groups=mesh['data'=1,'cp'=2,'tp'=4] {'cp','tp'}, dimensions={0} | all-to-all | bytes 16777216 | tf_op jit(solution)/shard_map/all_to_all | solution.py:122
  623.0 0.0 copy-done.8
  623.0 9.4 %multiply_reduce_fusion = f32[512,2048]{1,0:T(8,128)S(1)} fusion(f32[512,2]{0,1:T(2,128)S(1)} %copy-done.8, bf16[2048,2048,1]{1,0,2:T(8,128)(2,1)S(1)} %bitcast.110, s32[512,2]{0,1:T(2,128)S(1)} %multiply_add_fusion), kind=kOutput, calls=%fused_computation.6 | convolution fusion | flops 8595177472 | bytes 12591104 | tf_op jit(solution)/shard_map/tkn,nm->tkm/dot_general | solution.py:123
  632.4 0.0 copy-done.4
  632.4 2.5 add_convert_fusion
  634.9 0.0 copy-done.1
  (11 shorter events, 0.1 us)
Async XLA Ops:
  6.5 60.9 %copy-start = (bf16[2048,1,128]{2,0,1:T(8,128)(2,1)S(1)}, bf16[2048,1,128]{2,0,1:T(8,128)(2,1)}, u32[]{:S(2)}) copy-start(bf16[2048,1,128]{2,0,1:T(8,128)(2,1)} %param.13) | copy-start | bytes 1572868
  6.5 60.9 %all-gather.4.cloned.1.call-start = ((), (), s32[]{:S(2)}) async-start(), calls=%async_computation.3 | async-start | bytes 10485760 | tf_op jit(solution)/shard_map/all_gather | solution.py:98
  7.3 66.1 %copy-start.7 = (bf16[2048,1,128]{2,0,1:T(8,128)(2,1)S(1)}, bf16[2048,1,128]{2,0,1:T(8,128)(2,1)}, u32[]{:S(2)}) copy-start(bf16[2048,1,128]{2,0,1:T(8,128)(2,1)} %param.12) | copy-start | bytes 1572868
  7.3 99.9 %all-gather.6.cloned.1.call-start = ((), (), s32[]{:S(2)}) async-start(), calls=%async_computation.5 | async-start | bytes 3145728 | tf_op jit(solution)/shard_map/all_gather | solution.py:102
  67.4 5.9 copy-start.6
  76.8 263.8 %reduce-scatter.2.cloned.1.call-start = ((), (), s32[]{:S(2)}) async-start(), calls=%async_computation.4 | async-start | bytes 20971520 | tf_op jit(solution)/shard_map/reduce_scatter | solution.py:107
  221.7 0.7 copy-start.5
  222.4 118.2 %copy-start.3 = (bf16[512,2048]{1,0:T(8,128)(2,1)S(1)}, bf16[512,2048]{1,0:T(8,128)(2,1)}, u32[]{:S(2)}) copy-start(bf16[512,2048]{1,0:T(8,128)(2,1)} %param.10) | copy-start | bytes 6291460
  447.6 3.2 copy-start.2
  526.5 96.5 %copy-start.8 = (f32[512,2]{0,1:T(2,128)S(1)}, f32[512,2]{0,1:T(2,128)}, u32[]{:S(2)}) copy-start(f32[512,2]{0,1:T(2,128)} %param.16) | copy-start | bytes 12292
  623.0 9.5 %copy-start.4 = (f32[512,2048]{1,0:T(8,128)S(1)}, f32[512,2048]{1,0:T(8,128)}, u32[]{:S(2)}) copy-start(f32[512,2048]{1,0:T(8,128)} %reduce-scatter.2.cloned.1.call-done) | copy-start | bytes 12582916
  623.0 12.0 %copy-start.1 = (bf16[2048,1,128]{2,0,1:T(8,128)(2,1)S(1)}, bf16[2048,1,128]{2,0,1:T(8,128)(2,1)}, u32[]{:S(2)}) copy-start(bf16[2048,1,128]{2,0,1:T(8,128)(2,1)} %param.13) | copy-start | bytes 1572868
Sparse Core Ops, SparseCore 0:
  8.9 58.5 all-gather.3
  77.0 30.1 all-gather.5
  221.9 118.7 reduce-scatter.1

commit v2 on v1

--- a/solution.py
+++ b/solution.py
@@ -9,7 +9,8 @@
 QB = 256
 KB = 512
 LOG2E = 1.4426950408889634
-VLIM = 62 * 1024 * 1024
+VLIM = 60 * 1024 * 1024
+MESH = pl.DeviceIdType.MESH
 
 
 def attend_block(q_of, k_ref, v_ref, m_ref, l_ref, acc_ref, pos0, heads, hd):
@@ -22,13 +23,19 @@
         start = pl.multiple_of(kb * KB, KB)
         k = k_ref[pl.ds(start, KB), :]
         v = v_ref[pl.ds(start, KB), :]
+        score = lambda h: lax.dot_general(q_of(h), k, (((1,), (1,)), ((), ())), preferred_element_type=jnp.float32)
+        if masked:
+            qp = pos0 + lax.broadcasted_iota(jnp.int32, (QB, KB), 0)
+            kp = start + lax.broadcasted_iota(jnp.int32, (QB, KB), 1)
+            keep = kp <= qp
+        s_next = score(0)
         for h in range(heads):
             rows = slice(h * QB, (h + 1) * QB)
-            s = lax.dot_general(q_of(h), k, (((1,), (1,)), ((), ())), preferred_element_type=jnp.float32)
+            s = s_next
+            if h + 1 < heads:
+                s_next = score(h + 1)
             if masked:
-                qp = pos0 + lax.broadcasted_iota(jnp.int32, (QB, KB), 0)
-                kp = start + lax.broadcasted_iota(jnp.int32, (QB, KB), 1)
-                s = jnp.where(kp <= qp, s, -jnp.inf)
+                s = jnp.where(keep, s, -jnp.inf)
             m_old = m_ref[rows, :]
             m_new = jnp.maximum(m_old, jnp.max(s, axis=1, keepdims=True))
             alpha = jnp.exp2((m_old - m_new) * c)
@@ -65,6 +72,110 @@
     o_ref[...] = jnp.dot(ob_ref[...], wo_ref[...], preferred_element_type=jnp.float32)
 
 
+def moe_kernel(num_devs, tp_size, exp_local, cap, h_ref, slot_ref, idx_ref, gate_ref, wg_ref, wu_ref, wd_ref, y_ref, hbuf, tok, wgb, wub, wdb, zrecv, yacc, hsem, wsem, send_sem, recv_sem):
+    rows, width = y_ref.shape
+    local_slots = exp_local * cap
+    me = lax.axis_index('cp') * tp_size + lax.axis_index('tp')
+    groups = recv_sem.shape[0]
+    per_group = exp_local // groups
+
+    barrier = pltpu.get_barrier_semaphore()
+    for j in range(1, num_devs):
+        other = lax.rem(me + j, num_devs)
+        pl.semaphore_signal(barrier, inc=1, device_id=(0, other // tp_size, lax.rem(other, tp_size)), device_id_type=MESH)
+    pl.semaphore_wait(barrier, num_devs - 1)
+
+    def weight_copies(e, slot):
+        return [pltpu.make_async_copy(src.at[e], dst.at[slot], wsem.at[i, slot]) for i, (src, dst) in enumerate(((wg_ref, wgb), (wu_ref, wub), (wd_ref, wdb)))]
+
+    def h_copy(s, slot):
+        return pltpu.make_async_copy(h_ref.at[pl.ds(pl.multiple_of(s * rows, rows), rows)], hbuf.at[slot], hsem.at[slot])
+
+    h_copy(0, 0).start()
+    for e in range(2):
+        for copy in weight_copies(e, e):
+            copy.start()
+
+    def pick(s, carry):
+        slot = lax.rem(s, 2)
+        h_copy(s, slot).wait()
+
+        @pl.when(s + 1 < num_devs)
+        def _():
+            h_copy(s + 1, 1 - slot).start()
+
+        ids = slot_ref[s] - me * local_slots
+        want = lax.broadcasted_iota(jnp.int32, (local_slots, rows), 0)
+        sel = jnp.logical_or(ids[0:1, :] == want, ids[1:2, :] == want)
+        sel = jnp.where(sel, 1.0, 0.0).astype(jnp.bfloat16)
+        at = pl.multiple_of(s * cap, cap)
+        for c0 in range(0, width, 512):
+            part = jnp.dot(sel, hbuf[slot, :, c0:c0 + 512], preferred_element_type=jnp.float32).astype(jnp.bfloat16)
+            tok[:, pl.ds(at, cap), c0:c0 + 512] = part.reshape(exp_local, cap, 512)
+
+        @pl.when(s == me)
+        def _():
+            yacc[...] = hbuf[slot].astype(jnp.float32)
+
+        return carry
+
+    lax.fori_loop(0, num_devs, pick, 0)
+
+    def expert(e, carry):
+        slot = lax.rem(e, 2)
+        for copy in weight_copies(e, slot):
+            copy.wait()
+        x = tok[e]
+        gate = jnp.dot(x, wgb[slot], preferred_element_type=jnp.float32)
+        up = jnp.dot(x, wub[slot], preferred_element_type=jnp.float32)
+        act = (jax.nn.silu(gate) * up).astype(jnp.bfloat16)
+        tok[e] = jnp.dot(act, wdb[slot], preferred_element_type=jnp.float32).astype(jnp.bfloat16)
+        group = e // per_group
+        for j in range(1, num_devs):
+            other = lax.rem(me + j, num_devs)
+            pltpu.make_async_remote_copy(
+                src_ref=tok.at[e, pl.ds(pl.multiple_of(other * cap, cap), cap)],
+                dst_ref=zrecv.at[e, pl.ds(pl.multiple_of(me * cap, cap), cap)],
+                send_sem=send_sem,
+                recv_sem=recv_sem.at[group],
+                device_id=(0, other // tp_size, lax.rem(other, tp_size)),
+                device_id_type=MESH,
+            ).start()
+        at = pl.ds(pl.multiple_of(me * cap, cap), cap)
+        zrecv[e, at, :] = tok[e, at, :]
+
+        @pl.when(e + 2 < exp_local)
+        def _():
+            for copy in weight_copies(e + 2, slot):
+                copy.start()
+
+        return carry
+
+    lax.fori_loop(0, exp_local, expert, 0)
+
+    span = per_group * num_devs * cap
+    back = per_group * (num_devs - 1) * cap
+
+    def combine(g, carry):
+        whole = zrecv.at[pl.ds(0, per_group), pl.ds(0, (num_devs - 1) * cap)]
+        pltpu.make_async_copy(whole, whole, recv_sem.at[g]).wait()
+        want = lax.broadcasted_iota(jnp.int32, (rows, span), 1) + g * span
+        sel0 = jnp.where(idx_ref[:, 0:1] == want, 1.0, 0.0).astype(jnp.bfloat16)
+        sel1 = jnp.where(idx_ref[:, 1:2] == want, 1.0, 0.0).astype(jnp.bfloat16)
+        first = pl.multiple_of(g * per_group, per_group)
+        for c0 in range(0, width, 512):
+            z = zrecv[pl.ds(first, per_group), :, c0:c0 + 512].reshape(span, 512)
+            z0 = jnp.dot(sel0, z, preferred_element_type=jnp.float32)
+            z1 = jnp.dot(sel1, z, preferred_element_type=jnp.float32)
+            yacc[:, c0:c0 + 512] += gate_ref[:, 0:1] * z0 + gate_ref[:, 1:2] * z1
+        return carry
+
+    lax.fori_loop(0, groups, combine, 0)
+    y_ref[...] = yacc[...].astype(y_ref.dtype)
+    sent = tok.at[:, pl.ds(0, (num_devs - 1) * cap)]
+    pltpu.make_async_copy(sent, sent, send_sem).wait()
+
+
 def solution(mesh):
     cp_size = mesh.shape['cp']
     tp_size = mesh.shape['tp']
@@ -88,6 +199,23 @@
             name='attn',
         )(queries, keys, vals, w_o)
 
+    def experts(h_all, slots_all, back_idx, gates, w_gate, w_up, w_down, cap):
+        rows, width = back_idx.shape[0], h_all.shape[1]
+        exp_local, _, ff = w_gate.shape
+        vmem = pl.BlockSpec(memory_space=pltpu.VMEM)
+        hbm = pl.BlockSpec(memory_space=pl.ANY)
+        bf16 = jnp.bfloat16
+        dma = pltpu.SemaphoreType.DMA
+        return pl.pallas_call(
+            functools.partial(moe_kernel, num_devs, tp_size, exp_local, cap),
+            in_specs=[hbm, vmem, vmem, vmem, hbm, hbm, hbm],
+            out_specs=vmem,
+            out_shape=jax.ShapeDtypeStruct((rows, width), bf16),
+            scratch_shapes=[pltpu.VMEM((2, rows, width), bf16), pltpu.VMEM((exp_local, num_devs * cap, width), bf16), pltpu.VMEM((2, width, ff), bf16), pltpu.VMEM((2, width, ff), bf16), pltpu.VMEM((2, ff, width), bf16), pltpu.VMEM((exp_local, num_devs * cap, width), bf16), pltpu.VMEM((rows, width), jnp.float32), dma((2,)), dma((3, 2)), dma, dma((4,))],
+            compiler_params=pltpu.CompilerParams(collective_id=2, has_side_effects=True, vmem_limit_bytes=VLIM),
+            name='moe',
+        )(h_all, slots_all, back_idx, gates, w_gate, w_up, w_down)
+
     def device_fn(x_blk, w_q, w_k, w_v, w_o, idx_blk, gate_blk, w_gate, w_up, w_down):
         tok_dev, width = x_blk.shape
         heads, head_dim = w_q.shape[1], w_k.shape[2]
@@ -111,17 +239,9 @@
         onehot = (flat_ids[:, None] == jnp.arange(num_exp)[None, :]).astype(jnp.int32)
         slot_pos = jnp.sum(jnp.cumsum(onehot, axis=0) * onehot, axis=1) - 1
         slot_ids = (flat_ids * capacity + slot_pos).reshape(tok_dev, 2)
-        select = (slot_ids[:, :, None] == jnp.arange(num_exp * capacity)[None, None, :]).astype(jnp.bfloat16)
-        send_buf = jnp.einsum('tkn,tm->nm', select, hidden, preferred_element_type=jnp.float32).astype(jnp.bfloat16)
-        recv_buf = lax.all_to_all(send_buf, ('cp', 'tp'), 0, 0, tiled=True)
-        tok_in = recv_buf.reshape(num_devs, exp_local, capacity, -1)
-        gate_pre = jnp.einsum('secm,emf->secf', tok_in, w_gate, preferred_element_type=jnp.float32)
-        up_pre = jnp.einsum('secm,emf->secf', tok_in, w_up, preferred_element_type=jnp.float32)
-        hid_act = (jax.nn.silu(gate_pre) * up_pre).astype(jnp.bfloat16)
-        exp_out = jnp.einsum('secf,efm->secm', hid_act, w_down, preferred_element_type=jnp.float32).astype(jnp.bfloat16)
-        back_buf = lax.all_to_all(exp_out.reshape(num_devs * exp_local * capacity, -1), ('cp', 'tp'), 0, 0, tiled=True)
-        picked = jnp.einsum('tkn,nm->tkm', select, back_buf, preferred_element_type=jnp.float32)
-        moe_out = jnp.sum(gate_blk[:, :, None] * picked, axis=1)
-        return (hidden.astype(jnp.float32) + moe_out).astype(jnp.bfloat16)
+        slots_all = lax.all_gather(slot_ids.T, ('cp', 'tp'), axis=0)
+        back_idx = (slot_ids // capacity % exp_local) * (num_devs * capacity) + slot_ids // (capacity * exp_local) * capacity + slot_ids % capacity
+        h_all = lax.all_gather(hidden, ('cp', 'tp'), axis=0, tiled=True)
+        return experts(h_all, slots_all, back_idx, gate_blk, w_gate, w_up, w_down, capacity)
 
     return jax.shard_map(device_fn, mesh=mesh, in_specs=(row_spec, head_spec, head_spec, head_spec, wo_spec, row_spec, row_spec, expert_spec, expert_spec, expert_spec), out_specs=row_spec, check_vma=False)

time: 642 us -> 523 us (0.81)
  blocking collectives: 193 us -> 11.8 us
  matrix products: 110 us -> 22.1 us
  Pallas kernels: 111 us -> 195 us
  waiting for transfers between devices: 191 us -> 265 us
  local copies, waits for them, and re-layouts: 16.3 us -> 8.33 us
    all_to_all x2 -> x0, blocking collectives: 193 us -> none  [the longest x1 96.5 us: device_fn(): lax.all_to_all(exp_out.reshape(num_devs * exp_local * capacity, -1), ('cp...]
    pallas_call x0 -> x1, Pallas kernels: none -> 118 us  [experts(): pl.pallas_call(functools.partial(moe_kernel, num_devs, tp_size, exp_local...]
    dot_general x4 -> x0, matrix products: 87.5 us -> none  [the longest x1 47.2 us: device_fn(): jnp.einsum('secf,efm->secm', hid_act, w_down, preferred_element_type=jnp....]
    all_gather x0 -> x1, waiting for transfers between devices: none -> 69 us  [device_fn(): h_all = lax.all_gather(hidden, ('cp', 'tp'), axis=0, tiled=True)]
    pallas_call x1, Pallas kernels: 111 us -> 77.3 us  [attention(): pl.pallas_call(functools.partial(attn_kernel, cp_size, tp_size, heads, hd...]
    all_gather x0 -> x1, blocking collectives: none -> 11.8 us  [device_fn(): slots_all = lax.all_gather(slot_ids.T, ('cp', 'tp'), axis=0)]
    convert_element_type x1 -> x0, local copies, waits for them, and re-layouts: 8.27 us -> none  [device_fn(): jnp.einsum('secf,efm->secm', hid_act, w_down, preferred_element_type=jnp....]
  transfers between devices with their start and end apart: 3 -> 4, of which waited for: 3 -> 4; matrix products, arithmetic and copies ran while one was open for 3% -> 3% of each run, Pallas kernels for 0% -> 0%
where the time goes in v2:
time: 523 us
  waiting for transfers between devices  265 us (51%)
  Pallas kernels  195 us (37%)
  matrix products  22.1 us (4%)
  between operations  13.3 us (3%)
  blocking collectives  11.8 us (2%)
  local copies, waits for them, and re-layouts  8.33 us (2%)
  other arithmetic  7.31 us (1%)
    reduce_scatter x1, waiting for transfers between devices, device_fn(): attn_out = lax.psum_scatter(part_sum, 'tp', scatter_dimension=0, tiled=True)  119 us
    pallas_call x1, Pallas kernels, experts(): pl.pallas_call(functools.partial(moe_kernel, num_devs, tp_size, exp_local...  118 us
    pallas_call x1, Pallas kernels, attention(): pl.pallas_call(functools.partial(attn_kernel, cp_size, tp_size, heads, hd...  77.3 us
    all_gather x1, waiting for transfers between devices, device_fn(): h_all = lax.all_gather(hidden, ('cp', 'tp'), axis=0, tiled=True)  69 us
    all_gather x1, waiting for transfers between devices, device_fn(): x_rows = lax.all_gather(x_blk, 'tp', axis=0, tiled=True)  60.1 us
    dot_general x3, matrix products, device_fn(): jnp.dot(a, w.reshape(width, -1), preferred_element_type=jnp.float32)  22.1 us
    all_gather x1, waiting for transfers between devices, device_fn(): kv_all = lax.all_gather(kv_loc, 'cp', axis=0)  16.3 us
    all_gather x1, blocking collectives, device_fn(): slots_all = lax.all_gather(slot_ids.T, ('cp', 'tp'), axis=0)  11.8 us
  transfers between devices with their start and end apart: 4, of which 4 were waited for; matrix products, arithmetic and copies ran while one was open for 3% of the time, Pallas kernels for 0%

profile of v2, /device:TPU:0, one launch (start us, length us, event | category | flops | bytes accessed | tf_op | source)
XLA Modules:
  0.0 523.0 jit_solution(919042585344168806)
XLA Ops:
  6.5 0.0 copy-start
  6.5 0.0 all-gather.7.cloned.1.call-start
  6.5 0.7 all-gather.7.cloned.1.call-update
  7.3 0.0 copy-start.6
  7.3 0.0 all-gather.11.cloned.1.call-start
  7.3 60.1 %all-gather.7.cloned.1.call-done = bf16[2048,2048]{1,0:T(8,128)(2,1)} async-done(((bf16[512,2048]{1,0:T(8,128)(2,1)}), bf16[2048,2048]{1,0:T(8,128)(2,1)}) %all-gather.7.cloned.1.call-update) | async-done | bytes 8388624 | tf_op jit(solution)/shard_map/all_gather | solution.py:226
  67.4 0.0 copy-done
  67.4 0.0 copy-start.5
  67.5 5.9 %fusion.6 = bf16[1,2048,128]{2,1,0:T(8,128)(2,1)S(1)} fusion(bf16[2048,2048]{1,0:T(8,128)(2,1)} %all-gather.7.cloned.1.call-done, bf16[2048,1,128]{2,0,1:T(8,128)(2,1)S(1)} %copy-done), kind=kOutput, calls=%fused_computation.7 | convolution fusion | flops 1074003968 | bytes 9437184 | tf_op jit(solution)/shard_map/dot_general | solution.py:227
  73.3 0.0 copy-done.6
  73.3 0.0 copy-done.5
  73.3 2.4 fusion.7
  75.8 1.1 pad_maximum_fusion.1
  76.8 0.0 all-gather.11.cloned.1.call-update
  76.8 0.2 reduce-scatter.2.cloned.1.call-start
  77.1 13.8 %fusion.3.q_ref = bf16[2048,1024]{1,0:T(8,128)(2,1)} fusion(bf16[2048,2048]{1,0:T(8,128)(2,1)} %all-gather.7.cloned.1.call-done, bf16[256,8,8,128]{3,2,1,0:T(8,128)(2,1)} %bitcast.55), kind=kOutput, calls=%fused_computation.4 | convolution fusion | flops 8592031744 | bytes 16777216 | tf_op jit(solution)/shard_map/dot_general | solution.py:227
  90.9 16.3 %all-gather.11.cloned.1.call-done = bf16[4,2048,128]{2,1,0:T(8,128)(2,1)} async-done(((bf16[2,2048,128]{2,1,0:T(8,128)(2,1)}), bf16[4,2048,128]{2,1,0:T(8,128)(2,1)}) %all-gather.11.cloned.1.call-update) | async-done | bytes 2097168 | tf_op jit(solution)/shard_map/all_gather | solution.py:230
  107.1 1.7 slice_bitcast_fusion.3
  108.8 0.3 pad_maximum_fusion
  109.1 1.4 fusion.24
  110.5 77.3 %attn.1 = f32[2048,2048]{1,0:T(8,128)} custom-call(bf16[2048,1024]{1,0:T(8,128)(2,1)} %fusion.3.q_ref, bf16[4096,128]{1,0:T(8,128)(2,1)} %bitcast.53, bf16[4096,128]{1,0:T(8,128)(2,1)} %bitcast.52, bf16[1024,2048]{1,0:T(8,128)(2,1)} %bitcast.51), custom_call_target="tpu_custom_call" | custom-call | tf_op jit(solution)/shard_map/attn/pallas_call | solution.py:192
  187.9 0.0 copy-start.2
  187.9 0.0 reduce-scatter.2.cloned.1.call-update
  187.9 0.0 copy-start.3
  187.9 0.0 all-gather.9.cloned.1.call-start
  188.0 118.8 %reduce-scatter.2.cloned.1.call-done = f32[512,2048]{1,0:T(8,128)} async-done(((f32[2048,2048]{1,0:T(8,128)}), f32[512,2048]{1,0:T(8,128)}) %reduce-scatter.2.cloned.1.call-update) | async-done | bytes 4194320 | tf_op jit(solution)/shard_map/reduce_scatter | solution.py:235
  306.8 0.0 copy-done.2
  306.8 4.2 add_convert_fusion
  311.0 0.0 all-gather.9.cloned.1.call-update
  311.0 0.0 copy-done.3
  311.0 0.1 copy.36
  311.2 0.2 eq.32
  311.3 0.2 eq.28
  311.5 0.1 copy.38
  311.6 0.2 fusion.11
  311.9 0.1 copy.39
  312.0 0.4 fusion.8
  312.4 0.2 sub.17
  312.6 0.1 copy.40
  312.8 1.2 fusion.16
  313.9 0.1 copy.41
  314.0 0.0 copy-done.4
  314.0 0.9 copy.42.gate_ref
  314.9 11.8 %all-gather.2.slot_ref = s32[8,2,512]{2,1,0:T(2,128)} all-gather(s32[1,2,512]{2,1,0:T(2,128)S(1)} %copy.41), channel_id=3, replica_groups=mesh['data'=1,'cp'=2,'tp'=4] {'cp','tp'}, dimensions={0}, use_global_device_ids=true | all-gather | bytes 36864 | tf_op jit(solution)/shard_map/all_gather | solution.py:242
  326.7 69.0 %all-gather.9.cloned.1.call-done.h_ref = bf16[4096,2048]{1,0:T(8,128)(2,1)} async-done(((bf16[512,2048]{1,0:T(8,128)(2,1)}), bf16[4096,2048]{1,0:T(8,128)(2,1)}) %all-gather.9.cloned.1.call-update) | async-done | bytes 16777232 | tf_op jit(solution)/shard_map/all_gather | solution.py:244
  395.7 117.6 %moe.1 = bf16[512,2048]{1,0:T(8,128)(2,1)} custom-call(bf16[4096,2048]{1,0:T(8,128)(2,1)} %all-gather.9.cloned.1.call-done.h_ref, s32[8,2,512]{2,1,0:T(2,128)} %all-gather.2.slot_ref, s32[512,2]{1,0:T(8,128)} %get-tuple-element.11.idx_ref, f32[512,2]{1,0:T(8,128)} %copy.42.gate_ref, bf16[16,2048,768]{2,1,0:T(8,128)(2,1)} %wg_ref.1, ...), custom_call_target="tpu_custom_call" | custom-call | tf_op jit(solution)/shard_map/moe/pallas_call | solution.py:209
  513.3 3.2 copy.55
  516.5 0.0 copy-done.1
  (8 shorter events, 0.1 us)
Async XLA Ops:
  6.5 60.9 %copy-start = (bf16[2048,1,128]{2,0,1:T(8,128)(2,1)S(1)}, bf16[2048,1,128]{2,0,1:T(8,128)(2,1)}, u32[]{:S(2)}) copy-start(bf16[2048,1,128]{2,0,1:T(8,128)(2,1)} %param.12) | copy-start | bytes 1572868
  6.5 60.9 %all-gather.7.cloned.1.call-start = ((), (), s32[]{:S(2)}) async-start(), calls=%async_computation.1 | async-start | bytes 10485760 | tf_op jit(solution)/shard_map/all_gather | solution.py:226
  7.3 66.1 %copy-start.6 = (bf16[2048,1,128]{2,0,1:T(8,128)(2,1)S(1)}, bf16[2048,1,128]{2,0,1:T(8,128)(2,1)}, u32[]{:S(2)}) copy-start(bf16[2048,1,128]{2,0,1:T(8,128)(2,1)} %param.13) | copy-start | bytes 1572868
  7.3 99.9 %all-gather.11.cloned.1.call-start = ((), (), s32[]{:S(2)}) async-start(), calls=%async_computation.4 | async-start | bytes 3145728 | tf_op jit(solution)/shard_map/all_gather | solution.py:230
  67.4 5.9 %copy-start.5 = (bf16[2048,2048]{1,0:T(8,128)(2,1)S(1)}, bf16[2048,2048]{1,0:T(8,128)(2,1)}, u32[]{:S(2)}) copy-start(bf16[2048,2048]{1,0:T(8,128)(2,1)} %all-gather.7.cloned.1.call-done) | copy-start | bytes 25165828
  76.8 229.9 %reduce-scatter.2.cloned.1.call-start = ((), (), s32[]{:S(2)}) async-start(), calls=%async_computation.2 | async-start | bytes 20971520 | tf_op jit(solution)/shard_map/reduce_scatter | solution.py:235
  187.9 118.9 %copy-start.2 = (bf16[512,2048]{1,0:T(8,128)(2,1)S(1)}, bf16[512,2048]{1,0:T(8,128)(2,1)}, u32[]{:S(2)}) copy-start(bf16[512,2048]{1,0:T(8,128)(2,1)} %param.10) | copy-start | bytes 6291460
  187.9 123.1 %copy-start.3 = (s32[512,2]{0,1:T(2,128)S(1)}, s32[512,2]{0,1:T(2,128)}, u32[]{:S(2)}) copy-start(s32[512,2]{0,1:T(2,128)} %param.15) | copy-start | bytes 12292
  187.9 207.8 %all-gather.9.cloned.1.call-start = ((), (), s32[]{:S(2)}) async-start(), calls=%async_computation.3 | async-start | bytes 18874368 | tf_op jit(solution)/shard_map/all_gather | solution.py:244
  311.0 3.1 copy-start.4
  395.7 120.8 %copy-start.1 = (bf16[2048,1,128]{2,0,1:T(8,128)(2,1)S(1)}, bf16[2048,1,128]{2,0,1:T(8,128)(2,1)}, u32[]{:S(2)}) copy-start(bf16[2048,1,128]{2,0,1:T(8,128)(2,1)} %param.12) | copy-start | bytes 1572868
Sparse Core Ops, SparseCore 0:
  8.9 58.5 all-gather.6
  77.0 30.1 all-gather.10
  188.0 118.7 reduce-scatter.1
  311.1 84.5 all-gather.8

commit v3 on v2

--- a/solution.py
+++ b/solution.py
@@ -8,12 +8,13 @@
 
 QB = 256
 KB = 512
+CH = 128
 LOG2E = 1.4426950408889634
 VLIM = 60 * 1024 * 1024
 MESH = pl.DeviceIdType.MESH
 
 
-def attend_block(q_of, k_ref, v_ref, m_ref, l_ref, acc_ref, pos0, heads, hd):
+def attend_block(q_of, kv_ref, m_ref, l_ref, acc_ref, pos0, heads, hd):
     c = (hd ** -0.5) * LOG2E
     m_ref[...] = jnp.full(m_ref.shape, -jnp.inf, jnp.float32)
     l_ref[...] = jnp.zeros(l_ref.shape, jnp.float32)
@@ -21,8 +22,8 @@
 
     def step(kb, masked):
         start = pl.multiple_of(kb * KB, KB)
-        k = k_ref[pl.ds(start, KB), :]
-        v = v_ref[pl.ds(start, KB), :]
+        k = kv_ref[pl.ds(start, KB), :hd]
+        v = kv_ref[pl.ds(start, KB), hd:]
         score = lambda h: lax.dot_general(q_of(h), k, (((1,), (1,)), ((), ())), preferred_element_type=jnp.float32)
         if masked:
             qp = pos0 + lax.broadcasted_iota(jnp.int32, (QB, KB), 0)
@@ -57,19 +58,164 @@
     step(last, True)
 
 
-def attn_kernel(cp_size, tp_size, heads, hd, q_ref, k_ref, v_ref, wo_ref, o_ref, m_ref, l_ref, acc_ref, ob_ref):
-    b = pl.program_id(0)
-    r = lax.axis_index('cp')
-    t_src = b // 2
-    half = b % 2
-    seg = r + half * (2 * cp_size - 1 - 2 * r)
-    pos0 = (seg * tp_size + t_src) * QB
-    attend_block(lambda h: q_ref[:, h * hd:(h + 1) * hd], k_ref, v_ref, m_ref, l_ref, acc_ref, pos0, heads, hd)
-    for h in range(heads):
-        rows = slice(h * QB, (h + 1) * QB)
-        den = jnp.sum(l_ref[rows, :], axis=1, keepdims=True)
-        ob_ref[:, h * hd:(h + 1) * hd] = (acc_ref[rows, :] / den).astype(jnp.bfloat16)
-    o_ref[...] = jnp.dot(ob_ref[...], wo_ref[...], preferred_element_type=jnp.float32)
+def rdma(src, dst, send_sem, recv_sem, cp, tp):
+    return pltpu.make_async_remote_copy(src_ref=src, dst_ref=dst, send_sem=send_sem, recv_sem=recv_sem, device_id=(0, cp, tp), device_id_type=MESH)
+
+
+def await_bytes(ref, sem):
+    pltpu.make_async_copy(ref, ref, sem).wait()
+
+
+def greet(others):
+    barrier = pltpu.get_barrier_semaphore()
+    for cp, tp in others:
+        pl.semaphore_signal(barrier, inc=1, device_id=(0, cp, tp), device_id_type=MESH)
+    pl.semaphore_wait(barrier, len(others))
+
+
+def qkv_kernel(cp_size, tp_size, x_ref, slot_ref, wq_ref, wk_ref, wv_ref, q_ref, kv_ref, slots_ref, x_all, wq, wkv, wsem, slot_send, slot_recv, own_send, x_recv, near_recv, fwd_send, fwd_recv, kv_send, kv_recv, slot_sem):
+    r, t = lax.axis_index('cp'), lax.axis_index('tp')
+    num_devs = cp_size * tp_size
+    me = r * tp_size + t
+    near = t + 1 - 2 * lax.rem(t, 2)
+    far = lax.rem(t + 2, tp_size)
+    far_near = lax.rem(near + 2, tp_size)
+    peer = 1 - r
+    rows = x_ref.shape[0]
+    half_rows = rows // 2
+    hd = wk_ref.shape[1]
+    devs = [lax.rem(me + j, num_devs) for j in range(1, num_devs)]
+
+    weights = [pltpu.make_async_copy(wk_ref, wkv.at[:, pl.ds(0, hd)], wsem.at[0]), pltpu.make_async_copy(wv_ref, wkv.at[:, pl.ds(hd, hd)], wsem.at[1]), pltpu.make_async_copy(wq_ref, wq, wsem.at[2])]
+    for copy in weights:
+        copy.start()
+    greet([(d // tp_size, lax.rem(d, tp_size)) for d in devs])
+    chunks = rows // CH
+    for j in range(chunks):
+        at = pl.ds(j * CH, CH)
+        rdma(x_ref.at[at], x_all.at[t, at], own_send, x_recv.at[j], r, far).start()
+    rdma(x_ref, x_all.at[t], own_send, near_recv, r, near).start()
+    for d in devs:
+        rdma(slot_ref, slots_ref.at[me], slot_send, slot_recv, d // tp_size, lax.rem(d, tp_size)).start()
+    mine = pltpu.make_async_copy(slot_ref, slots_ref.at[me], slot_sem)
+    mine.start()
+    for copy in weights:
+        copy.wait()
+
+    def project(x, tp_src, row0, count):
+        half = row0 // half_rows
+        seg = r + half * (2 * cp_size - 1 - 2 * r)
+        pos = pl.multiple_of((seg * tp_size + tp_src) * half_rows + row0 % half_rows, CH)
+        kv_ref[pl.ds(pos, count), :] = jnp.dot(x, wkv[...], preferred_element_type=jnp.float32).astype(jnp.bfloat16)
+        sent = kv_ref.at[pl.ds(pos, count)]
+        rdma(sent, sent, kv_send, kv_recv, peer, t).start()
+        at = pl.ds(pl.multiple_of(tp_src * rows + row0, CH), count)
+        q_ref[at, :] = jnp.dot(x, wq[...], preferred_element_type=jnp.float32).astype(jnp.bfloat16)
+
+    for half in range(2):
+        project(x_ref[half * half_rows:(half + 1) * half_rows, :], t, half * half_rows, half_rows)
+    await_bytes(x_all.at[near], near_recv)
+    for half in range(2):
+        project(x_all[near, half * half_rows:(half + 1) * half_rows, :], near, half * half_rows, half_rows)
+    for j in range(chunks):
+        at = pl.ds(j * CH, CH)
+        await_bytes(x_all.at[far, at], x_recv.at[j])
+        rdma(x_all.at[far, at], x_all.at[far, at], fwd_send, fwd_recv.at[j], r, near).start()
+        project(x_all[far, j * CH:(j + 1) * CH, :], far, j * CH, CH)
+        await_bytes(x_all.at[far_near, at], fwd_recv.at[j])
+        project(x_all[far_near, j * CH:(j + 1) * CH, :], far_near, j * CH, CH)
+
+    mine.wait()
+    await_bytes(slots_ref.at[pl.ds(0, num_devs - 1)], slot_recv)
+    await_bytes(slots_ref.at[pl.ds(0, num_devs - 1)], slot_send)
+    await_bytes(x_all.at[pl.ds(0, 2)], own_send)
+    await_bytes(x_all.at[0], fwd_send)
+    half_kv = kv_ref.at[pl.ds(0, tp_size * rows)]
+    await_bytes(half_kv, kv_recv)
+    await_bytes(half_kv, kv_send)
+
+
+def block_kernel(cp_size, tp_size, heads, hd, q_ref, kv_ref, wo_ref, x_ref, h_ref, m_ref, l_ref, acc_ref, ob_ref, part, from_near, from_far, hbuf, near_send, near_recv, far_send, far_recv, h_send, h_near, h_far, h_peer, h_diag, h_own):
+    r, t = lax.axis_index('cp'), lax.axis_index('tp')
+    me = r * tp_size + t
+    near = t + 1 - 2 * lax.rem(t, 2)
+    far = lax.rem(t + 2, tp_size)
+    peer = 1 - r
+    rows, width = x_ref.shape
+    greet([(r, near), (r, far), (peer, t)])
+
+    def block(i, carry):
+        local = i // 4
+        mine = lax.rem(i, 2)
+        half = lax.rem(i // 2, 2)
+        t_dst = lax.rem(mine * t + (1 - mine) * near + 2 * (1 - local), tp_size)
+        seg = r + half * (2 * cp_size - 1 - 2 * r)
+        pos0 = (seg * tp_size + t_dst) * QB
+        row0 = pl.multiple_of(t_dst * rows + half * QB, QB)
+        attend_block(lambda h: q_ref[pl.ds(row0, QB), h * hd:(h + 1) * hd], kv_ref, m_ref, l_ref, acc_ref, pos0, heads, hd)
+        for h in range(heads):
+            at = slice(h * QB, (h + 1) * QB)
+            den = jnp.sum(l_ref[at, :], axis=1, keepdims=True)
+            ob_ref[:, h * hd:(h + 1) * hd] = (acc_ref[at, :] / den).astype(jnp.bfloat16)
+        part[i] = jnp.dot(ob_ref[...], wo_ref[...], preferred_element_type=jnp.float32)
+
+        @pl.when(mine == 0)
+        def _():
+            rdma(part.at[i], from_near.at[i // 2], near_send, near_recv.at[i // 2], r, near).start()
+
+        @pl.when(jnp.logical_and(mine == 1, local == 0))
+        def _():
+            await_bytes(from_near.at[half], near_recv.at[half])
+            part[i] += from_near[half]
+            for c in range(QB // CH):
+                at = pl.ds(c * CH, CH)
+                rdma(part.at[i, at], from_far.at[half, at], far_send, far_recv.at[half, c], r, far).start()
+
+        return carry
+
+    lax.fori_loop(0, 8, block, 0)
+
+    def h_rows(cp, tp, j):
+        return h_ref.at[pl.ds(pl.multiple_of((cp * tp_size + tp) * rows + j * CH, CH), CH)]
+
+    per_half = QB // CH
+    chunks = rows // CH
+    for j in range(chunks):
+        half, c = j // per_half, j % per_half
+        at = slice(c * CH, (c + 1) * CH)
+        if c == 0:
+            await_bytes(from_near.at[2 + half], near_recv.at[2 + half])
+        await_bytes(from_far.at[half, pl.ds(c * CH, CH)], far_recv.at[half, c])
+        total = part[5 + 2 * half, at, :] + from_near[2 + half, at, :] + from_far[half, at, :]
+        hbuf[j] = (x_ref[j * CH:(j + 1) * CH, :].astype(jnp.float32) + total).astype(jnp.bfloat16)
+        mine = h_rows(r, t, j)
+        rdma(hbuf.at[j], mine, h_send, h_far.at[j], r, far).start()
+        rdma(hbuf.at[j], mine, h_send, h_peer.at[j], peer, t).start()
+        rdma(hbuf.at[j], mine, h_send, h_near, r, near).start()
+        pltpu.make_async_copy(hbuf.at[j], mine, h_own).start()
+        got = h_rows(peer, t, j)
+        await_bytes(got, h_peer.at[j])
+        rdma(got, got, h_send, h_near, r, near).start()
+
+    def diag(j):
+        got = h_rows(peer, far, j)
+        await_bytes(got, h_diag.at[j])
+        rdma(got, got, h_send, h_near, r, near).start()
+
+    for j in range(chunks):
+        got = h_rows(r, far, j)
+        await_bytes(got, h_far.at[j])
+        rdma(got, got, h_send, h_diag.at[j], peer, t).start()
+        rdma(got, got, h_send, h_near, r, near).start()
+        if j > 0:
+            diag(j - 1)
+    diag(chunks - 1)
+
+    await_bytes(h_ref.at[pl.ds(0, 4 * rows)], h_near)
+    await_bytes(h_ref.at[pl.ds(0, 7 * rows)], h_send)
+    await_bytes(h_ref.at[pl.ds(0, rows)], h_own)
+    await_bytes(part.at[pl.ds(0, 4)], near_send)
+    await_bytes(part.at[pl.ds(0, 2)], far_send)
 
 
 def moe_kernel(num_devs, tp_size, exp_local, cap, h_ref, slot_ref, idx_ref, gate_ref, wg_ref, wu_ref, wd_ref, y_ref, hbuf, tok, wgb, wub, wdb, zrecv, yacc, hsem, wsem, send_sem, recv_sem):
@@ -185,34 +331,52 @@
     wo_spec = P('tp', None, None)
     expert_spec = P(('cp', 'tp'), None, None)
 
-    def attention(queries, keys, vals, w_o, heads, hd):
-        rows, width = queries.shape[0], w_o.shape[1]
-        seq = keys.shape[0]
-        full = lambda shape: pl.BlockSpec(shape, lambda b: (0, 0))
+    vmem = pl.BlockSpec(memory_space=pltpu.VMEM)
+    hbm = pl.BlockSpec(memory_space=pl.ANY)
+    dma = pltpu.SemaphoreType.DMA
+    bf16, f32 = jnp.bfloat16, jnp.float32
+
+    def params(number):
+        return pltpu.CompilerParams(collective_id=number, has_side_effects=True, vmem_limit_bytes=VLIM)
+
+    def project(x_blk, slot_ids, w_q, w_k, w_v):
+        rows, width = x_blk.shape
+        q_width, kv_width = w_q.shape[1], w_k.shape[1]
+        group = rows * tp_size
         return pl.pallas_call(
-            functools.partial(attn_kernel, cp_size, tp_size, heads, hd),
-            grid=(rows // QB,),
-            in_specs=[pl.BlockSpec((QB, heads * hd), lambda b: (b, 0)), full((seq, hd)), full((seq, hd)), full((heads * hd, width))],
-            out_specs=pl.BlockSpec((QB, width), lambda b: (b, 0)),
-            out_shape=jax.ShapeDtypeStruct((rows, width), jnp.float32),
-            scratch_shapes=[pltpu.VMEM((heads * QB, 128), jnp.float32), pltpu.VMEM((heads * QB, 128), jnp.float32), pltpu.VMEM((heads * QB, hd), jnp.float32), pltpu.VMEM((QB, heads * hd), jnp.bfloat16)],
+            functools.partial(qkv_kernel, cp_size, tp_size),
+            in_specs=[vmem, vmem, hbm, hbm, hbm],
+            out_specs=[vmem, vmem, vmem],
+            out_shape=[jax.ShapeDtypeStruct((group, q_width), bf16), jax.ShapeDtypeStruct((group * cp_size, 2 * kv_width), bf16), jax.ShapeDtypeStruct((num_devs,) + slot_ids.shape, jnp.int32)],
+            scratch_shapes=[pltpu.VMEM((tp_size, rows, width), bf16), pltpu.VMEM((width, q_width), bf16), pltpu.VMEM((width, 2 * kv_width), bf16), dma((3,)), dma, dma, dma, dma((rows // CH,)), dma, dma, dma((rows // CH,)), dma, dma, dma],
+            compiler_params=params(0),
+            name='qkv',
+        )(x_blk, slot_ids, w_q, w_k, w_v)
+
+    def attention(q, kv, w_o, x_blk, heads, hd):
+        rows, width = x_blk.shape
+        v32 = lambda *shape: pltpu.VMEM(shape, f32)
+        chunks = rows // CH
+        return pl.pallas_call(
+            functools.partial(block_kernel, cp_size, tp_size, heads, hd),
+            in_specs=[vmem, vmem, vmem, vmem],
+            out_specs=hbm,
+            out_shape=jax.ShapeDtypeStruct((rows * num_devs, width), bf16),
+            scratch_shapes=[v32(heads * QB, 128), v32(heads * QB, 128), v32(heads * QB, hd), pltpu.VMEM((QB, heads * hd), bf16), v32(8, QB, width), v32(4, QB, width), v32(2, QB, width), pltpu.VMEM((chunks, CH, width), bf16), dma, dma((4,)), dma, dma((2, QB // CH)), dma, dma, dma((chunks,)), dma((chunks,)), dma((chunks,)), dma],
+            compiler_params=params(1),
             name='attn',
-        )(queries, keys, vals, w_o)
+        )(q, kv, w_o, x_blk)
 
     def experts(h_all, slots_all, back_idx, gates, w_gate, w_up, w_down, cap):
         rows, width = back_idx.shape[0], h_all.shape[1]
         exp_local, _, ff = w_gate.shape
-        vmem = pl.BlockSpec(memory_space=pltpu.VMEM)
-        hbm = pl.BlockSpec(memory_space=pl.ANY)
-        bf16 = jnp.bfloat16
-        dma = pltpu.SemaphoreType.DMA
         return pl.pallas_call(
             functools.partial(moe_kernel, num_devs, tp_size, exp_local, cap),
             in_specs=[hbm, vmem, vmem, vmem, hbm, hbm, hbm],
             out_specs=vmem,
             out_shape=jax.ShapeDtypeStruct((rows, width), bf16),
             scratch_shapes=[pltpu.VMEM((2, rows, width), bf16), pltpu.VMEM((exp_local, num_devs * cap, width), bf16), pltpu.VMEM((2, width, ff), bf16), pltpu.VMEM((2, width, ff), bf16), pltpu.VMEM((2, ff, width), bf16), pltpu.VMEM((exp_local, num_devs * cap, width), bf16), pltpu.VMEM((rows, width), jnp.float32), dma((2,)), dma((3, 2)), dma, dma((4,))],
-            compiler_params=pltpu.CompilerParams(collective_id=2, has_side_effects=True, vmem_limit_bytes=VLIM),
+            compiler_params=params(2),
             name='moe',
         )(h_all, slots_all, back_idx, gates, w_gate, w_up, w_down)
 
@@ -223,25 +387,14 @@
         num_exp = exp_local * num_devs
         capacity = 4 * tok_dev // num_exp
 
-        x_rows = lax.all_gather(x_blk, 'tp', axis=0, tiled=True)
-        mm = lambda a, w: jnp.dot(a, w.reshape(width, -1), preferred_element_type=jnp.float32).astype(jnp.bfloat16)
-        queries = mm(x_rows, w_q)
-        kv_loc = jnp.stack([mm(x_rows, w_k), mm(x_rows, w_v)])
-        kv_all = lax.all_gather(kv_loc, 'cp', axis=0)
-        kv_all = kv_all.reshape(cp_size, 2, tp_size, 2, QB, head_dim)
-        order = [kv_all[s, :, :, 0] for s in range(cp_size)] + [kv_all[cp_size - 1 - s, :, :, 1] for s in range(cp_size)]
-        kv_pos = jnp.stack(order, axis=1).reshape(2, -1, head_dim)
-        part_sum = attention(queries, kv_pos[0], kv_pos[1], w_o.reshape(heads * head_dim, width), heads, head_dim)
-        attn_out = lax.psum_scatter(part_sum, 'tp', scatter_dimension=0, tiled=True)
-        hidden = (x_blk.astype(jnp.float32) + attn_out).astype(jnp.bfloat16)
-
         flat_ids = idx_blk.reshape(-1)
         onehot = (flat_ids[:, None] == jnp.arange(num_exp)[None, :]).astype(jnp.int32)
         slot_pos = jnp.sum(jnp.cumsum(onehot, axis=0) * onehot, axis=1) - 1
         slot_ids = (flat_ids * capacity + slot_pos).reshape(tok_dev, 2)
-        slots_all = lax.all_gather(slot_ids.T, ('cp', 'tp'), axis=0)
         back_idx = (slot_ids // capacity % exp_local) * (num_devs * capacity) + slot_ids // (capacity * exp_local) * capacity + slot_ids % capacity
-        h_all = lax.all_gather(hidden, ('cp', 'tp'), axis=0, tiled=True)
+        flat = lambda w: w.reshape(width, -1)
+        q, kv, slots_all = project(x_blk, slot_ids.T, flat(w_q), flat(w_k), flat(w_v))
+        h_all = attention(q, kv, w_o.reshape(heads * head_dim, width), x_blk, heads, head_dim)
         return experts(h_all, slots_all, back_idx, gate_blk, w_gate, w_up, w_down, capacity)
 
     return jax.shard_map(device_fn, mesh=mesh, in_specs=(row_spec, head_spec, head_spec, head_spec, wo_spec, row_spec, row_spec, expert_spec, expert_spec, expert_spec), out_specs=row_spec, check_vma=False)

time: 523 us -> 371 us (0.71)
  waiting for transfers between devices: 265 us -> 0 us
  Pallas kernels: 195 us -> 357 us
  matrix products: 22.1 us -> 0 us
  between operations: 13.3 us -> 0.13 us
  blocking collectives: 11.8 us -> 0 us
  other arithmetic: 7.31 us -> 1.82 us
    pallas_call x1 -> x2, Pallas kernels: 77.3 us -> 236 us  [the longest x1 176 us: attention(): pl.pallas_call(functools.partial(block_kernel, cp_size, tp_size, heads, h...]
    all_gather x3 -> x0, waiting for transfers between devices: 145 us -> none  [the longest x1 69 us: device_fn(): h_all = lax.all_gather(hidden, ('cp', 'tp'), axis=0, tiled=True)]
    reduce_scatter x1 -> x0, waiting for transfers between devices: 119 us -> none  [device_fn(): attn_out = lax.psum_scatter(part_sum, 'tp', scatter_dimension=0, tiled=True)]
    dot_general x3 -> x0, matrix products: 22.1 us -> none  [device_fn(): jnp.dot(a, w.reshape(width, -1), preferred_element_type=jnp.float32)]
    all_gather x1 -> x0, blocking collectives: 11.8 us -> none  [device_fn(): slots_all = lax.all_gather(slot_ids.T, ('cp', 'tp'), axis=0)]
    unnamed x18 -> x8, local copies, waits for them, and re-layouts: 4.32 us -> 10.1 us
  transfers between devices with their start and end apart: 4 -> 0, of which waited for: 4 -> 0; matrix products, arithmetic and copies ran while one was open for 3% -> 0% of each run, Pallas kernels for 0% -> 0%
where the time goes in v3:
time: 371 us
  Pallas kernels  357 us (96%)
  local copies, waits for them, and re-layouts  11.7 us (3%)
    pallas_call x1, Pallas kernels, attention(): pl.pallas_call(functools.partial(block_kernel, cp_size, tp_size, heads, h...  176 us
    pallas_call x1, Pallas kernels, experts(): pl.pallas_call(functools.partial(moe_kernel, num_devs, tp_size, exp_local...  121 us
    pallas_call x1, Pallas kernels, project(): pl.pallas_call(functools.partial(qkv_kernel, cp_size, tp_size), in_specs=...  60.2 us
    unnamed x8, local copies, waits for them, and re-layouts  10.1 us

profile of v3, /device:TPU:0, one launch (start us, length us, event | category | flops | bytes accessed | tf_op | source)
XLA Modules:
  0.0 371.0 jit_solution(3028318169701746835)
XLA Ops:
  0.0 0.0 copy-start
  0.0 0.9 copy.16
  0.9 0.2 eq.32
  1.1 0.1 copy.18
  1.2 0.2 fusion.1
  1.5 0.1 copy.19
  1.6 0.2 eq.28
  1.8 0.4 fusion
  2.1 0.2 sub.17
  2.3 0.0 copy-done
  2.4 0.1 copy.20
  2.5 1.2 fusion.6
  3.7 0.7 copy.21.slot_ref
  4.4 5.2 %copy.25 = bf16[256,8,8,128]{3,1,2,0:T(8,128)(2,1)} copy(bf16[256,8,8,128]{3,2,1,0:T(8,128)(2,1)} %bitcast.19) | data formatting | bytes 8388608
  9.6 60.2 %qkv.1 = (bf16[2048,1024]{1,0:T(8,128)(2,1)}, bf16[4096,256]{1,0:T(8,128)(2,1)}, s32[8,2,512]{2,1,0:T(2,128)}) custom-call(bf16[512,2048]{1,0:T(8,128)(2,1)} %x_ref.3, s32[2,512]{1,0:T(2,128)} %copy.21.slot_ref, bf16[2048,1024]{1,0:T(8,128)(2,1)} %bitcast.17, bf16[2048,128]{1,0:T(8,128)(2,1)} %bitcast.20, bf16[2048,128]{1,0:T(8,128)(2,1)} %bitcast.21), custom_call_target="tpu_custom_call" | custom-call | tf_op jit(solution)/shard_map/qkv/pallas_call | solution.py:346
  69.8 0.0 copy-start.1
  69.8 176.3 %attn.1.h_ref = bf16[4096,2048]{1,0:T(8,128)(2,1)} custom-call(bf16[2048,1024]{1,0:T(8,128)(2,1)} %get-tuple-element.8.q_ref, bf16[4096,256]{1,0:T(8,128)(2,1)} %get-tuple-element.9.kv_ref, bf16[1024,2048]{1,0:T(8,128)(2,1)} %bitcast.18, bf16[512,2048]{1,0:T(8,128)(2,1)} %x_ref.3), custom_call_target="tpu_custom_call" | custom-call | tf_op jit(solution)/shard_map/attn/pallas_call | solution.py:360
  246.1 0.0 copy-done.1
  246.1 0.9 copy.22.gate_ref
  247.0 120.8 %moe.1 = bf16[512,2048]{1,0:T(8,128)(2,1)} custom-call(bf16[4096,2048]{1,0:T(8,128)(2,1)} %attn.1.h_ref, s32[8,2,512]{2,1,0:T(2,128)} %get-tuple-element.10.slot_ref, s32[512,2]{1,0:T(8,128)} %get-tuple-element.11.idx_ref, f32[512,2]{1,0:T(8,128)} %copy.22.gate_ref, bf16[16,2048,768]{2,1,0:T(8,128)(2,1)} %wg_ref.1, bf16[16,2048,768]{2,1,0:T(8,128)(2,1)} %wu_ref.1, ...), custom_call_target="tpu_custom_call" | custom-call | tf_op jit(solution)/shard_map/moe/pallas_call | solution.py:373
  367.8 3.2 copy.27
  (6 shorter events, 0.1 us)
Async XLA Ops:
  0.0 2.3 copy-start
  69.8 176.3 %copy-start.1 = (f32[512,2]{0,1:T(2,128)S(1)}, f32[512,2]{0,1:T(2,128)}, u32[]{:S(2)}) copy-start(f32[512,2]{0,1:T(2,128)} %param.16) | copy-start | bytes 12292

commit v4 on v3

v4 whole, which is shorter than its diff:
```python
import functools
import jax
import jax.numpy as jnp
from jax import lax
from jax.experimental import pallas as pl
from jax.experimental.pallas import tpu as pltpu
from jax.sharding import PartitionSpec as P

QB = 256
KB = 512
CH = 128
HC = 64
LOG2E = 1.4426950408889634
VLIM = 60 * 1024 * 1024
MESH = pl.DeviceIdType.MESH


def attend_block(q_of, kv_ref, m_ref, l_ref, acc_ref, pos0, heads, hd):
    c = (hd ** -0.5) * LOG2E
    m_ref[...] = jnp.full(m_ref.shape, -jnp.inf, jnp.float32)
    l_ref[...] = jnp.zeros(l_ref.shape, jnp.float32)
    acc_ref[...] = jnp.zeros(acc_ref.shape, jnp.float32)

    def step(kb, masked):
        start = pl.multiple_of(kb * KB, KB)
        k = kv_ref[pl.ds(start, KB), :hd]
        v = kv_ref[pl.ds(start, KB), hd:]
        score = lambda h: lax.dot_general(q_of(h), k, (((1,), (1,)), ((), ())), preferred_element_type=jnp.float32)
        if masked:
            qp = pos0 + lax.broadcasted_iota(jnp.int32, (QB, KB), 0)
            kp = start + lax.broadcasted_iota(jnp.int32, (QB, KB), 1)
            keep = kp <= qp
        s_next = score(0)
        for h in range(heads):
            rows = slice(h * QB, (h + 1) * QB)
            s = s_next
            if h + 1 < heads:
                s_next = score(h + 1)
            if masked:
                s = jnp.where(keep, s, -jnp.inf)
            m_old = m_ref[rows, :]
            m_new = jnp.maximum(m_old, jnp.max(s, axis=1, keepdims=True))
            alpha = jnp.exp2((m_old - m_new) * c)
            p = jnp.exp2((s - jnp.concatenate([m_new] * (KB // 128), axis=1)) * c)
            lp = p[:, :128]
            for j in range(1, KB // 128):
                lp = lp + p[:, j * 128:(j + 1) * 128]
            m_ref[rows, :] = m_new
            l_ref[rows, :] = l_ref[rows, :] * alpha + lp
            acc_ref[rows, :] = acc_ref[rows, :] * alpha + jnp.dot(p.astype(jnp.bfloat16), v, preferred_element_type=jnp.float32)

    last = pos0 // KB

    def body(kb, carry):
        step(kb, False)
        return carry

    lax.fori_loop(0, last, body, 0)
    step(last, True)


def rdma(src, dst, send_sem, recv_sem, cp, tp):
    return pltpu.make_async_remote_copy(src_ref=src, dst_ref=dst, send_sem=send_sem, recv_sem=recv_sem, device_id=(0, cp, tp), device_id_type=MESH)


def await_bytes(ref, sem):
    pltpu.make_async_copy(ref, ref, sem).wait()


def greet(others):
    barrier = pltpu.get_barrier_semaphore()
    for cp, tp in others:
        pl.semaphore_signal(barrier, inc=1, device_id=(0, cp, tp), device_id_type=MESH)
    pl.semaphore_wait(barrier, len(others))


def slot_rows(idx_ref, num_exp, cap):
    rows = idx_ref.shape[1]
    expert = lax.broadcasted_iota(jnp.int32, (num_exp, rows), 0)
    hot = [jnp.where(idx_ref[k:k + 1, :] == expert, 1.0, 0.0) for k in range(2)]
    earlier = lax.broadcasted_iota(jnp.int32, (rows, rows), 0) < lax.broadcasted_iota(jnp.int32, (rows, rows), 1)
    earlier = jnp.where(earlier, 1.0, 0.0).astype(jnp.bfloat16)
    count = jnp.dot((hot[0] + hot[1]).astype(jnp.bfloat16), earlier, preferred_element_type=jnp.float32)
    return [idx_ref[k:k + 1, :] * cap + jnp.sum(hot[k] * count, axis=0, keepdims=True).astype(jnp.int32) for k in range(2)]


def front_kernel(cp_size, tp_size, heads, hd, num_exp, cap, x_ref, idx_ref, wq_ref, wk_ref, wv_ref, wo_ref, h_ref, tok_ref, hbuf, own_slots,
                 x_all, wq, wkv, wo, q_ref, kv_ref, slots, m_ref, l_ref, acc_ref, ob_ref, part, from_near, from_far,
                 wsem, slot_send, slot_recv, x_send, x_near, x_far, x_fwd_send, x_fwd, kv_send, kv_recv,
                 near_send, near_recv, far_send, far_recv, h_send, h_near, h_far, h_peer, h_diag, load_sem, tok_sem):
    r, t = lax.axis_index('cp'), lax.axis_index('tp')
    num_devs = cp_size * tp_size
    me = r * tp_size + t
    near = t + 1 - 2 * lax.rem(t, 2)
    far = lax.rem(t + 2, tp_size)
    far_near = lax.rem(near + 2, tp_size)
    peer = 1 - r
    rows, width = x_ref.shape
    half_rows = rows // 2
    devs = [lax.rem(me + j, num_devs) for j in range(1, num_devs)]

    weights = [pltpu.make_async_copy(wk_ref, wkv.at[:, pl.ds(0, hd)], wsem.at[0]), pltpu.make_async_copy(wv_ref, wkv.at[:, pl.ds(hd, hd)], wsem.at[1]), pltpu.make_async_copy(wq_ref, wq, wsem.at[2]), pltpu.make_async_copy(wo_ref, wo, wsem.at[3])]
    for copy in weights:
        copy.start()
    greet([(d // tp_size, lax.rem(d, tp_size)) for d in devs])
    chunks = rows // CH
    for j in range(chunks):
        at = pl.ds(j * CH, CH)
        rdma(x_ref.at[at], x_all.at[0, at], x_send, x_far.at[j], r, far).start()
    rdma(x_ref, x_all.at[1], x_send, x_near, r, near).start()
    mine = slot_rows(idx_ref, num_exp, cap)
    own_slots[...] = jnp.concatenate(mine + [jnp.zeros((6, rows), jnp.int32)], axis=0)
    slots[me] = own_slots[...]
    for d in devs:
        rdma(own_slots, slots.at[me], slot_send, slot_recv, d // tp_size, lax.rem(d, tp_size)).start()
    for copy in weights[:3]:
        copy.wait()

    def project(x, tp_src, row0, count):
        half = row0 // half_rows
        seg = r + half * (2 * cp_size - 1 - 2 * r)
        pos = pl.multiple_of((seg * tp_size + tp_src) * half_rows + row0 % half_rows, CH)
        kv_ref[pl.ds(pos, count), :] = jnp.dot(x, wkv[...], preferred_element_type=jnp.float32).astype(jnp.bfloat16)
        sent = kv_ref.at[pl.ds(pos, count)]
        rdma(sent, sent, kv_send, kv_recv.at[half], peer, t).start()
        at = pl.ds(pl.multiple_of(tp_src * rows + row0, CH), count)
        q_ref[at, :] = jnp.dot(x, wq[...], preferred_element_type=jnp.float32).astype(jnp.bfloat16)

    def project_far(half):
        for j in range(half * (chunks // 2), (half + 1) * (chunks // 2)):
            at = pl.ds(j * CH, CH)
            await_bytes(x_all.at[0, at], x_far.at[j])
            rdma(x_all.at[0, at], x_all.at[2, at], x_fwd_send, x_fwd.at[j], r, near).start()
            project(x_all[0, j * CH:(j + 1) * CH, :], far, j * CH, CH)
            await_bytes(x_all.at[2, at], x_fwd.at[j])
            project(x_all[2, j * CH:(j + 1) * CH, :], far_near, j * CH, CH)
        await_bytes(kv_ref.at[pl.ds(0, tp_size * half_rows)], kv_recv.at[half])

    for half in range(2):
        project(x_ref[half * half_rows:(half + 1) * half_rows, :], t, half * half_rows, half_rows)
    await_bytes(x_all.at[1], x_near)
    for half in range(2):
        project(x_all[1, half * half_rows:(half + 1) * half_rows, :], near, half * half_rows, half_rows)
    project_far(0)
    weights[3].wait()

    def block(i, carry):
        local = i // 4
        mine = lax.rem(i, 2)
        half = lax.rem(i // 2, 2)
        slot = mine * (2 + 2 * local) + half

        @pl.when(i == 2)
        def _():
            project_far(1)

        @pl.when(jnp.logical_and(mine == 0, local == 1))
        def _():
            await_bytes(part.at[half], near_send.at[half])

        t_dst = lax.rem(mine * t + (1 - mine) * near + 2 * (1 - local), tp_size)
        seg = r + half * (2 * cp_size - 1 - 2 * r)
        pos0 = (seg * tp_size + t_dst) * QB
        row0 = pl.multiple_of(t_dst * rows + half * QB, QB)
        attend_block(lambda h: q_ref[pl.ds(row0, QB), h * hd:(h + 1) * hd], kv_ref, m_ref, l_ref, acc_ref, pos0, heads, hd)
        for h in range(heads):
            at = slice(h * QB, (h + 1) * QB)
            den = jnp.sum(l_ref[at, :], axis=1, keepdims=True)
            ob_ref[:, h * hd:(h + 1) * hd] = (acc_ref[at, :] / den).astype(jnp.bfloat16)
        part[slot] = jnp.dot(ob_ref[...], wo[...], preferred_element_type=jnp.float32)

        @pl.when(mine == 0)
        def _():
            rdma(part.at[slot], from_near.at[i // 2], near_send.at[half], near_recv.at[i // 2], r, near).start()

        @pl.when(jnp.logical_and(mine == 1, local == 0))
        def _():
            await_bytes(from_near.at[half], near_recv.at[half])
            part[slot] += from_near[half]
            for c in range(QB // CH):
                at = pl.ds(c * CH, CH)
                rdma(part.at[slot, at], from_far.at[half, at], far_send, far_recv.at[half, c], r, far).start()

        return carry

    lax.fori_loop(0, 8, block, 0)
    await_bytes(x_all.at[0], x_fwd_send)

    def h_rows(cp, tp, j):
        return h_ref.at[pl.ds(pl.multiple_of((cp * tp_size + tp) * rows + j * HC, HC), HC)]

    def h_block(cp, tp):
        return h_ref.at[pl.ds(pl.multiple_of((cp * tp_size + tp) * rows, rows), rows)]

    OWN, PEER, FAR, DIAG = range(4)
    h_chunks = rows // HC
    for j in range(h_chunks):
        first = j * HC
        half, within = first // QB, first % QB
        at = slice(within, within + HC)
        if within == 0:
            await_bytes(from_near.at[2 + half], near_recv.at[2 + half])
        if within % CH == 0:
            await_bytes(from_far.at[half, pl.ds(within, CH)], far_recv.at[half, within // CH])
        total = part[4 + half, at, :] + from_near[2 + half, at, :] + from_far[half, at, :]
        hbuf[first:first + HC, :] = (x_ref[first:first + HC, :].astype(jnp.float32) + total).astype(jnp.bfloat16)
        src = hbuf.at[pl.ds(first, HC)]
        mine = h_rows(r, t, j)
        rdma(src, mine, h_send, h_far.at[j], r, far).start()
        rdma(src, mine, h_send, h_peer.at[j], peer, t).start()
        rdma(src, mine, h_send, h_near.at[OWN], r, near).start()

    await_bytes(slots.at[pl.ds(0, num_devs - 1)], slot_recv)
    local_slots = (num_exp // num_devs) * cap

    def pick(n, dev, src):
        ids = slots[dev] - me * local_slots
        want = lax.broadcasted_iota(jnp.int32, (local_slots, rows), 0)
        sel = jnp.logical_or(ids[0:1, :] == want, ids[1:2, :] == want)
        sel = jnp.where(sel, 1.0, 0.0).astype(jnp.bfloat16)
        stage = x_all.at[2, pl.ds((n % 2) * local_slots, local_slots)]
        out = lambda k: [pltpu.make_async_copy(x_all.at[2, pl.ds((k % 2) * local_slots + e * cap, cap)], tok_ref.at[e, pl.ds(pl.multiple_of(dev * cap, cap), cap)], tok_sem.at[k % 2]) for e in range(num_exp // num_devs)]
        if n >= 2:
            await_bytes(stage, tok_sem.at[n % 2])
        for c0 in range(0, width, 512):
            stage[:, c0:c0 + 512] = jnp.dot(sel, src[:, c0:c0 + 512], preferred_element_type=jnp.float32).astype(jnp.bfloat16)
        for copy in out(n):
            copy.start()

    def fetch(n, cp, tp):
        return pltpu.make_async_copy(h_block(cp, tp), x_all.at[n % 2], load_sem.at[n % 2])

    def forward(got, kind):
        rdma(got, got, h_send, h_near.at[kind], r, near).start()

    pick(0, me, hbuf)
    for j in range(h_chunks):
        got = h_rows(peer, t, j)
        await_bytes(got, h_peer.at[j])
        forward(got, PEER)
    fetch(1, peer, t).start()
    fetch(1, peer, t).wait()
    pick(1, peer * tp_size + t, x_all.at[1])

    def diag(j):
        got = h_rows(peer, far, j)
        await_bytes(got, h_diag.at[j])
        forward(got, DIAG)

    for j in range(h_chunks):
        got = h_rows(r, far, j)
        await_bytes(got, h_far.at[j])
        rdma(got, got, h_send, h_diag.at[j], peer, t).start()
        forward(got, FAR)
        if j > 1:
            diag(j - 2)
        if j == 2:
            await_bytes(h_block(r, near), h_near.at[OWN])
            fetch(2, r, near).start()
            fetch(2, r, near).wait()
            pick(2, r * tp_size + near, x_all.at[0])
        if j == 4:
            await_bytes(h_block(peer, near), h_near.at[PEER])
            fetch(3, peer, near).start()
            fetch(3, peer, near).wait()
            pick(3, peer * tp_size + near, x_all.at[1])
    fetch(4, r, far).start()
    diag(h_chunks - 2)
    await_bytes(h_block(r, far_near), h_near.at[FAR])
    fetch(5, r, far_near).start()
    fetch(4, r, far).wait()
    pick(4, r * tp_size + far, x_all.at[0])
    fetch(5, r, far_near).wait()
    pick(5, r * tp_size + far_near, x_all.at[1])
    diag(h_chunks - 1)
    fetch(6, peer, far).start()
    await_bytes(h_block(peer, far_near), h_near.at[DIAG])
    fetch(7, peer, far_near).start()
    fetch(6, peer, far).wait()
    pick(6, peer * tp_size + far, x_all.at[0])
    fetch(7, peer, far_near).wait()
    pick(7, peer * tp_size + far_near, x_all.at[1])

    for n in range(2):
        await_bytes(x_all.at[2, pl.ds(0, local_slots)], tok_sem.at[n])
        await_bytes(part.at[n], near_send.at[n])
    await_bytes(h_ref.at[pl.ds(0, 7 * rows)], h_send)
    await_bytes(part.at[pl.ds(0, 2)], far_send)
    await_bytes(slots.at[pl.ds(0, num_devs - 1)], slot_send)
    await_bytes(x_all.at[pl.ds(0, 2)], x_send)
    await_bytes(kv_ref.at[pl.ds(0, tp_size * rows)], kv_send)


def moe_kernel(num_devs, tp_size, exp_local, cap, tok_ref, h_ref, slot_ref, gate_ref, wg_ref, wu_ref, wd_ref, y_ref, tok, wgb, wub, wdb, zrecv, yacc, cols, tsem, wsem, send_sem, recv_sem):
    rows, width = y_ref.shape
    local_slots = exp_local * cap
    me = lax.axis_index('cp') * tp_size + lax.axis_index('tp')
    groups = recv_sem.shape[0]
    per_group = exp_local // groups

    def weight_copies(e, slot):
        return [pltpu.make_async_copy(src.at[e], dst.at[slot], wsem.at[i, slot]) for i, (src, dst) in enumerate(((wg_ref, wgb), (wu_ref, wub), (wd_ref, wdb)))]

    loads = [pltpu.make_async_copy(tok_ref.at[at], tok.at[at], tsem.at[n]) for n, at in enumerate((pl.ds(0, 2), pl.ds(2, exp_local - 2)))]
    for e in range(2):
        loads[e].start()
        for copy in weight_copies(e, e):
            copy.start()
    greet([(lax.rem(me + j, num_devs) // tp_size, lax.rem(lax.rem(me + j, num_devs), tp_size)) for j in range(1, num_devs)])
    slot = slot_ref[0:2, :]
    back = (slot // cap % exp_local) * (num_devs * cap) + slot // local_slots * cap + slot % cap
    columns = jnp.concatenate([back.astype(jnp.float32), gate_ref[...], jnp.zeros((124, rows), jnp.float32)], axis=0)
    cols[...] = jnp.transpose(columns)
    yacc[...] = h_ref[...].astype(jnp.float32)
    loads[0].wait()

    def expert(e, carry):
        slot = lax.rem(e, 2)
        for copy in weight_copies(e, slot):
            copy.wait()

        @pl.when(e == 2)
        def _():
            loads[1].wait()

        x = tok[e]
        gate = jnp.dot(x, wgb[slot], preferred_element_type=jnp.float32)
        up = jnp.dot(x, wub[slot], preferred_element_type=jnp.float32)
        act = (jax.nn.silu(gate) * up).astype(jnp.bfloat16)
        tok[e] = jnp.dot(act, wdb[slot], preferred_element_type=jnp.float32).astype(jnp.bfloat16)
        group = e // per_group
        for j in range(1, num_devs):
            other = lax.rem(me + j, num_devs)
            rdma(tok.at[e, pl.ds(pl.multiple_of(other * cap, cap), cap)], zrecv.at[e, pl.ds(pl.multiple_of(me * cap, cap), cap)], send_sem, recv_sem.at[group], other // tp_size, lax.rem(other, tp_size)).start()
        at = pl.ds(pl.multiple_of(me * cap, cap), cap)
        zrecv[e, at, :] = tok[e, at, :]

        @pl.when(e + 2 < exp_local)
        def _():
            for copy in weight_copies(e + 2, slot):
                copy.start()

        return carry

    lax.fori_loop(0, exp_local, expert, 0)

    span = per_group * num_devs * cap

    def combine(g, carry):
        await_bytes(zrecv.at[pl.ds(0, per_group), pl.ds(0, (num_devs - 1) * cap)], recv_sem.at[g])
        want = (lax.broadcasted_iota(jnp.int32, (rows, span), 1) + g * span).astype(jnp.float32)
        sel0 = jnp.where(cols[:, 0:1] == want, 1.0, 0.0).astype(jnp.bfloat16)
        sel1 = jnp.where(cols[:, 1:2] == want, 1.0, 0.0).astype(jnp.bfloat16)
        first = pl.multiple_of(g * per_group, per_group)
        for c0 in range(0, width, 512):
            z = zrecv[pl.ds(first, per_group), :, c0:c0 + 512].reshape(span, 512)
            z0 = jnp.dot(sel0, z, preferred_element_type=jnp.float32)
            z1 = jnp.dot(sel1, z, preferred_element_type=jnp.float32)
            yacc[:, c0:c0 + 512] += cols[:, 2:3] * z0 + cols[:, 3:4] * z1
        return carry

    lax.fori_loop(0, groups, combine, 0)
    y_ref[...] = yacc[...].astype(y_ref.dtype)
    await_bytes(tok.at[:, pl.ds(0, (num_devs - 1) * cap)], send_sem)


def solution(mesh):
    cp_size = mesh.shape['cp']
    tp_size = mesh.shape['tp']
    num_devs = cp_size * tp_size
    row_spec = P(('data', 'cp', 'tp'), None)
    head_spec = P(None, 'tp', None)
    wo_spec = P('tp', None, None)
    expert_spec = P(('cp', 'tp'), None, None)

    vmem = pl.BlockSpec(memory_space=pltpu.VMEM)
    hbm = pl.BlockSpec(memory_space=pl.ANY)
    dma = pltpu.SemaphoreType.DMA
    bf16, f32 = jnp.bfloat16, jnp.float32

    def params(number):
        return pltpu.CompilerParams(collective_id=number, has_side_effects=True, vmem_limit_bytes=VLIM)

    def front(x_blk, idx, w_q, w_k, w_v, w_o, heads, hd, exp_local, cap):
        rows, width = x_blk.shape
        group = rows * tp_size
        v32 = lambda *shape: pltpu.VMEM(shape, f32)
        v16 = lambda *shape: pltpu.VMEM(shape, bf16)
        return pl.pallas_call(
            functools.partial(front_kernel, cp_size, tp_size, heads, hd, exp_local * num_devs, cap),
            in_specs=[vmem, vmem, hbm, hbm, hbm, hbm],
            out_specs=[hbm, hbm, vmem, vmem],
            out_shape=[jax.ShapeDtypeStruct((rows * num_devs, width), bf16), jax.ShapeDtypeStruct((exp_local, num_devs * cap, width), bf16), jax.ShapeDtypeStruct((rows, width), bf16), jax.ShapeDtypeStruct((8, rows), jnp.int32)],
            scratch_shapes=[
                v16(3, rows, width), v16(width, heads * hd), v16(width, 2 * hd), v16(heads * hd, width), v16(group, heads * hd), v16(group * cp_size, 2 * hd),
                pltpu.VMEM((num_devs, 8, rows), jnp.int32), v32(heads * QB, 128), v32(heads * QB, 128), v32(heads * QB, hd), v16(QB, heads * hd),
                v32(6, QB, width), v32(4, QB, width), v32(2, QB, width),
                dma((4,)), dma, dma, dma, dma, dma((rows // CH,)), dma, dma((rows // CH,)), dma, dma((2,)),
                dma((2,)), dma((4,)), dma, dma((2, QB // CH)), dma, dma((4,)), dma((rows // HC,)), dma((rows // HC,)), dma((rows // HC,)), dma((2,)), dma((2,))],
            compiler_params=params(0),
            name='front',
        )(x_blk, idx, w_q, w_k, w_v, w_o)

    def experts(tok, h_own, slots, gates, w_gate, w_up, w_down, cap):
        rows, width = h_own.shape
        exp_local, _, ff = w_gate.shape
        v16 = lambda *shape: pltpu.VMEM(shape, bf16)
        return pl.pallas_call(
            functools.partial(moe_kernel, num_devs, tp_size, exp_local, cap),
            in_specs=[hbm, vmem, vmem, vmem, hbm, hbm, hbm],
            out_specs=vmem,
            out_shape=jax.ShapeDtypeStruct((rows, width), bf16),
            scratch_shapes=[v16(exp_local, num_devs * cap, width), v16(2, width, ff), v16(2, width, ff), v16(2, ff, width), v16(exp_local, num_devs * cap, width), pltpu.VMEM((rows, width), f32), pltpu.VMEM((rows, 128), f32), dma((2,)), dma((3, 2)), dma, dma((4,))],
            compiler_params=params(1),
            name='moe',
        )(tok, h_own, slots, gates, w_gate, w_up, w_down)

    def device_fn(x_blk, w_q, w_k, w_v, w_o, idx_blk, gate_blk, w_gate, w_up, w_down):
        tok_dev, width = x_blk.shape
        heads, head_dim = w_q.shape[1], w_k.shape[2]
        exp_local = w_gate.shape[0]
        num_exp = exp_local * num_devs
        capacity = 4 * tok_dev // num_exp

        flat = lambda w: w.reshape(width, -1)
        _, tok, h_own, slots = front(x_blk, idx_blk.T, flat(w_q), flat(w_k), flat(w_v), w_o.reshape(heads * head_dim, width), heads, head_dim, exp_local, capacity)
        return experts(tok, h_own, slots, gate_blk.T, w_gate, w_up, w_down, capacity)

    return jax.shard_map(device_fn, mesh=mesh, in_specs=(row_spec, head_spec, head_spec, head_spec, wo_spec, row_spec, row_spec, expert_spec, expert_spec, expert_spec), out_specs=row_spec, check_vma=False)
```

time: 371 us -> 340 us (0.916)
  Pallas kernels: 357 us -> 331 us
    pallas_call x1, Pallas kernels: 121 us -> 105 us  [experts(): pl.pallas_call(functools.partial(moe_kernel, num_devs, tp_size, exp_local...]
    pallas_call x2 -> x1, Pallas kernels: 236 us -> 226 us  [front(): pl.pallas_call(functools.partial(front_kernel, cp_size, tp_size, heads, h...]
    unnamed x8 -> x2, local copies, waits for them, and re-layouts: 10.1 us -> 8.41 us
where the time goes in v4:
time: 340 us
  Pallas kernels  331 us (97%)
  local copies, waits for them, and re-layouts  8.41 us (2%)
    pallas_call x1, Pallas kernels, front(): pl.pallas_call(functools.partial(front_kernel, cp_size, tp_size, heads, h...  226 us
    pallas_call x1, Pallas kernels, experts(): pl.pallas_call(functools.partial(moe_kernel, num_devs, tp_size, exp_local...  105 us
    unnamed x2, local copies, waits for them, and re-layouts  8.41 us

profile of v4, /device:TPU:0, one launch (start us, length us, event | category | flops | bytes accessed | tf_op | source)
XLA Modules:
  0.0 339.7 jit_solution(6807064096339142170)
XLA Ops:
  0.0 5.3 %copy.13 = bf16[256,8,8,128]{3,1,2,0:T(8,128)(2,1)} copy(bf16[256,8,8,128]{3,2,1,0:T(8,128)(2,1)} %bitcast.10) | data formatting | bytes 8388608
  5.3 226.2 %front.1 = (bf16[4096,2048]{1,0:T(8,128)(2,1)}, bf16[16,128,2048]{2,1,0:T(8,128)(2,1)}, bf16[512,2048]{1,0:T(8,128)(2,1)}, s32[8,512]{1,0:T(8,128)}) custom-call(bf16[512,2048]{1,0:T(8,128)(2,1)} %x_ref.1, s32[2,512]{1,0:T(2,128)} %bitcast.15, bf16[2048,1024]{1,0:T(8,128)(2,1)} %bitcast.9, bf16[2048,128]{1,0:T(8,128)(2,1)} %bitcast.12, ...), custom_call_target="tpu_custom_call" | custom-call | tf_op jit(solution)/shard_map/front/pallas_call | solution.py:389
  231.5 105.0 %moe.1 = bf16[512,2048]{1,0:T(8,128)(2,1)} custom-call(bf16[16,128,2048]{2,1,0:T(8,128)(2,1)} %get-tuple-element.8.tok_ref, bf16[512,2048]{1,0:T(8,128)(2,1)} %get-tuple-element.9.h_ref, s32[8,512]{1,0:T(8,128)} %get-tuple-element.10.slot_ref, f32[2,512]{1,0:T(2,128)} %bitcast.14, bf16[16,2048,768]{2,1,0:T(8,128)(2,1)} %wg_ref.1, ...), custom_call_target="tpu_custom_call" | custom-call | tf_op jit(solution)/shard_map/moe/pallas_call | solution.py:408
  336.5 3.2 copy.15

commit v5 on v4

--- a/solution.py
+++ b/solution.py
@@ -10,6 +10,8 @@
 KB = 512
 CH = 128
 HC = 64
+XD = 2
+WR = 256
 LOG2E = 1.4426950408889634
 VLIM = 60 * 1024 * 1024
 MESH = pl.DeviceIdType.MESH
@@ -87,7 +89,7 @@
 def front_kernel(cp_size, tp_size, heads, hd, num_exp, cap, x_ref, idx_ref, wq_ref, wk_ref, wv_ref, wo_ref, h_ref, tok_ref, hbuf, own_slots,
                  x_all, wq, wkv, wo, q_ref, kv_ref, slots, m_ref, l_ref, acc_ref, ob_ref, part, from_near, from_far,
                  wsem, slot_send, slot_recv, x_send, x_near, x_far, x_fwd_send, x_fwd, kv_send, kv_recv,
-                 near_send, near_recv, far_send, far_recv, h_send, h_near, h_far, h_peer, h_diag, load_sem, tok_sem):
+                 near_send, near_recv, far_send, far_recv, h_send, h_near, h_far, h_peer, h_diag, load_sem, tok_sem, raw, raw_sem):
     r, t = lax.axis_index('cp'), lax.axis_index('tp')
     num_devs = cp_size * tp_size
     me = r * tp_size + t
@@ -99,9 +101,15 @@
     half_rows = rows // 2
     devs = [lax.rem(me + j, num_devs) for j in range(1, num_devs)]
 
-    weights = [pltpu.make_async_copy(wk_ref, wkv.at[:, pl.ds(0, hd)], wsem.at[0]), pltpu.make_async_copy(wv_ref, wkv.at[:, pl.ds(hd, hd)], wsem.at[1]), pltpu.make_async_copy(wq_ref, wq, wsem.at[2]), pltpu.make_async_copy(wo_ref, wo, wsem.at[3])]
+    weights = [pltpu.make_async_copy(wk_ref, wkv.at[:, pl.ds(0, hd)], wsem.at[0]), pltpu.make_async_copy(wv_ref, wkv.at[:, pl.ds(hd, hd)], wsem.at[1]), pltpu.make_async_copy(wo_ref, wo, wsem.at[2])]
     for copy in weights:
         copy.start()
+
+    def raw_copy(k, slot):
+        return pltpu.make_async_copy(wq_ref.at[pl.ds(pl.multiple_of(k * WR, WR), WR)], raw.at[slot], raw_sem.at[slot])
+
+    for k in range(2):
+        raw_copy(k, k).start()
     greet([(d // tp_size, lax.rem(d, tp_size)) for d in devs])
     chunks = rows // CH
     for j in range(chunks):
@@ -113,8 +121,23 @@
     slots[me] = own_slots[...]
     for d in devs:
         rdma(own_slots, slots.at[me], slot_send, slot_recv, d // tp_size, lax.rem(d, tp_size)).start()
-    for copy in weights[:3]:
+    for copy in weights[:2]:
         copy.wait()
+
+    def flatten(k, carry):
+        slot = lax.rem(k, 2)
+        raw_copy(k, slot).wait()
+        at = pl.ds(pl.multiple_of(k * WR, WR), WR)
+        for h in range(heads):
+            wq[at, h * hd:(h + 1) * hd] = raw[slot, :, h, :]
+
+        @pl.when(k + 2 < width // WR)
+        def _():
+            raw_copy(k + 2, slot).start()
+
+        return carry
+
+    lax.fori_loop(0, width // WR, flatten, 0)
 
     def project(x, tp_src, row0, count):
         half = row0 // half_rows
@@ -142,7 +165,32 @@
     for half in range(2):
         project(x_all[1, half * half_rows:(half + 1) * half_rows, :], near, half * half_rows, half_rows)
     project_far(0)
-    weights[3].wait()
+    weights[2].wait()
+
+    def h_rows(cp, tp, j):
+        return h_ref.at[pl.ds(pl.multiple_of((cp * tp_size + tp) * rows + j * HC, HC), HC)]
+
+    def h_block(cp, tp):
+        return h_ref.at[pl.ds(pl.multiple_of((cp * tp_size + tp) * rows, rows), rows)]
+
+    OWN, PEER, FAR, DIAG = range(4)
+    h_chunks = rows // HC
+
+    def finish(half):
+        await_bytes(from_near.at[2 + half], near_recv.at[2 + half])
+        for within in range(0, QB, HC):
+            first = half * QB + within
+            j = first // HC
+            at = slice(within, within + HC)
+            if within % CH == 0:
+                await_bytes(from_far.at[half, pl.ds(within, CH)], far_recv.at[half, within // CH])
+            total = part[4 + half, at, :] + from_near[2 + half, at, :] + from_far[half, at, :]
+            hbuf[first:first + HC, :] = (x_ref[first:first + HC, :].astype(jnp.float32) + total).astype(jnp.bfloat16)
+            src = hbuf.at[pl.ds(first, HC)]
+            mine = h_rows(r, t, j)
+            rdma(src, mine, h_send, h_far.at[j], r, far).start()
+            rdma(src, mine, h_send, h_peer.at[j], peer, t).start()
+            rdma(src, mine, h_send, h_near.at[OWN], r, near).start()
 
     def block(i, carry):
         local = i // 4
@@ -153,6 +201,10 @@
         @pl.when(i == 2)
         def _():
             project_far(1)
+
+        @pl.when(i == 6)
+        def _():
+            finish(0)
 
         @pl.when(jnp.logical_and(mine == 0, local == 1))
         def _():
@@ -186,30 +238,7 @@
     lax.fori_loop(0, 8, block, 0)
     await_bytes(x_all.at[0], x_fwd_send)
 
-    def h_rows(cp, tp, j):
-        return h_ref.at[pl.ds(pl.multiple_of((cp * tp_size + tp) * rows + j * HC, HC), HC)]
-
-    def h_block(cp, tp):
-        return h_ref.at[pl.ds(pl.multiple_of((cp * tp_size + tp) * rows, rows), rows)]
-
-    OWN, PEER, FAR, DIAG = range(4)
-    h_chunks = rows // HC
-    for j in range(h_chunks):
-        first = j * HC
-        half, within = first // QB, first % QB
-        at = slice(within, within + HC)
-        if within == 0:
-            await_bytes(from_near.at[2 + half], near_recv.at[2 + half])
-        if within % CH == 0:
-            await_bytes(from_far.at[half, pl.ds(within, CH)], far_recv.at[half, within // CH])
-        total = part[4 + half, at, :] + from_near[2 + half, at, :] + from_far[half, at, :]
-        hbuf[first:first + HC, :] = (x_ref[first:first + HC, :].astype(jnp.float32) + total).astype(jnp.bfloat16)
-        src = hbuf.at[pl.ds(first, HC)]
-        mine = h_rows(r, t, j)
-        rdma(src, mine, h_send, h_far.at[j], r, far).start()
-        rdma(src, mine, h_send, h_peer.at[j], peer, t).start()
-        rdma(src, mine, h_send, h_near.at[OWN], r, near).start()
-
+    finish(1)
     await_bytes(slots.at[pl.ds(0, num_devs - 1)], slot_recv)
     local_slots = (num_exp // num_devs) * cap
 
@@ -233,46 +262,61 @@
     def forward(got, kind):
         rdma(got, got, h_send, h_near.at[kind], r, near).start()
 
-    pick(0, me, hbuf)
-    for j in range(h_chunks):
-        got = h_rows(peer, t, j)
-        await_bytes(got, h_peer.at[j])
-        forward(got, PEER)
-    fetch(1, peer, t).start()
-    fetch(1, peer, t).wait()
-    pick(1, peer * tp_size + t, x_all.at[1])
-
     def diag(j):
         got = h_rows(peer, far, j)
         await_bytes(got, h_diag.at[j])
         forward(got, DIAG)
 
-    for j in range(h_chunks):
+    def from_peer(j):
+        got = h_rows(peer, t, j)
+        await_bytes(got, h_peer.at[j])
+        forward(got, PEER)
+        if j < XD:
+            rdma(got, got, h_send, h_diag.at[j], r, far).start()
+
+    def across(j):
         got = h_rows(r, far, j)
         await_bytes(got, h_far.at[j])
-        rdma(got, got, h_send, h_diag.at[j], peer, t).start()
         forward(got, FAR)
-        if j > 1:
-            diag(j - 2)
-        if j == 2:
-            await_bytes(h_block(r, near), h_near.at[OWN])
-            fetch(2, r, near).start()
-            fetch(2, r, near).wait()
-            pick(2, r * tp_size + near, x_all.at[0])
-        if j == 4:
-            await_bytes(h_block(peer, near), h_near.at[PEER])
-            fetch(3, peer, near).start()
-            fetch(3, peer, near).wait()
-            pick(3, peer * tp_size + near, x_all.at[1])
+        if j >= XD:
+            rdma(got, got, h_send, h_diag.at[j], peer, t).start()
+
+    for j in range(h_chunks // 2):
+        from_peer(j)
+    pick(0, me, hbuf)
+    for j in range(h_chunks // 2):
+        across(j)
+        from_peer(h_chunks // 2 + j)
+    fetch(1, peer, t).start()
+    fetch(1, peer, t).wait()
+    pick(1, peer * tp_size + t, x_all.at[1])
+    across(4)
+    diag(2)
+    diag(3)
+    await_bytes(h_block(r, near), h_near.at[OWN])
+    fetch(2, r, near).start()
+    fetch(2, r, near).wait()
+    pick(2, r * tp_size + near, x_all.at[0])
+    across(5)
+    await_bytes(h_block(peer, near), h_near.at[PEER])
+    fetch(3, peer, near).start()
+    fetch(3, peer, near).wait()
+    pick(3, peer * tp_size + near, x_all.at[1])
+    across(6)
+    diag(4)
+    across(7)
     fetch(4, r, far).start()
-    diag(h_chunks - 2)
+    diag(5)
     await_bytes(h_block(r, far_near), h_near.at[FAR])
     fetch(5, r, far_near).start()
     fetch(4, r, far).wait()
     pick(4, r * tp_size + far, x_all.at[0])
+    diag(6)
     fetch(5, r, far_near).wait()
     pick(5, r * tp_size + far_near, x_all.at[1])
-    diag(h_chunks - 1)
+    for j in range(XD):
+        diag(j)
+    diag(7)
     fetch(6, peer, far).start()
     await_bytes(h_block(peer, far_near), h_near.at[DIAG])
     fetch(7, peer, far_near).start()
@@ -395,8 +439,8 @@
                 v16(3, rows, width), v16(width, heads * hd), v16(width, 2 * hd), v16(heads * hd, width), v16(group, heads * hd), v16(group * cp_size, 2 * hd),
                 pltpu.VMEM((num_devs, 8, rows), jnp.int32), v32(heads * QB, 128), v32(heads * QB, 128), v32(heads * QB, hd), v16(QB, heads * hd),
                 v32(6, QB, width), v32(4, QB, width), v32(2, QB, width),
-                dma((4,)), dma, dma, dma, dma, dma((rows // CH,)), dma, dma((rows // CH,)), dma, dma((2,)),
-                dma((2,)), dma((4,)), dma, dma((2, QB // CH)), dma, dma((4,)), dma((rows // HC,)), dma((rows // HC,)), dma((rows // HC,)), dma((2,)), dma((2,))],
+                dma((3,)), dma, dma, dma, dma, dma((rows // CH,)), dma, dma((rows // CH,)), dma, dma((2,)),
+                dma((2,)), dma((4,)), dma, dma((2, QB // CH)), dma, dma((4,)), dma((rows // HC,)), dma((rows // HC,)), dma((rows // HC,)), dma((2,)), dma((2,)), v16(2, WR, heads, hd), dma((2,))],
             compiler_params=params(0),
             name='front',
         )(x_blk, idx, w_q, w_k, w_v, w_o)
@@ -423,7 +467,7 @@
         capacity = 4 * tok_dev // num_exp
 
         flat = lambda w: w.reshape(width, -1)
-        _, tok, h_own, slots = front(x_blk, idx_blk.T, flat(w_q), flat(w_k), flat(w_v), w_o.reshape(heads * head_dim, width), heads, head_dim, exp_local, capacity)
+        _, tok, h_own, slots = front(x_blk, idx_blk.T, w_q, flat(w_k), flat(w_v), w_o.reshape(heads * head_dim, width), heads, head_dim, exp_local, capacity)
         return experts(tok, h_own, slots, gate_blk.T, w_gate, w_up, w_down, capacity)
 
     return jax.shard_map(device_fn, mesh=mesh, in_specs=(row_spec, head_spec, head_spec, head_spec, wo_spec, row_spec, row_spec, expert_spec, expert_spec, expert_spec), out_specs=row_spec, check_vma=False)

time: 340 us -> 314 us (0.924)
  Pallas kernels: 331 us -> 310 us
  local copies, waits for them, and re-layouts: 8.41 us -> 3.16 us
    pallas_call x1, Pallas kernels: 226 us -> 206 us  [front(): pl.pallas_call(functools.partial(front_kernel, cp_size, tp_size, heads, h...]
    unnamed x2 -> x1, local copies, waits for them, and re-layouts: 8.41 us -> 3.16 us
where the time goes in v5:
time: 314 us; the launch traced here: 313 us
  Pallas kernels  310 us (99%)
  local copies, waits for them, and re-layouts  3.16 us (1%)
    pallas_call x1, Pallas kernels, front(): pl.pallas_call(functools.partial(front_kernel, cp_size, tp_size, heads, h...  206 us
    pallas_call x1, Pallas kernels, experts(): pl.pallas_call(functools.partial(moe_kernel, num_devs, tp_size, exp_local...  104 us

profile of v5, /device:TPU:0, one launch (start us, length us, event | category | flops | bytes accessed | tf_op | source)
XLA Modules:
  0.0 313.3 jit_solution(16934967061224937559)
XLA Ops:
  0.0 206.4 %front.1 = (bf16[4096,2048]{1,0:T(8,128)(2,1)}, bf16[16,128,2048]{2,1,0:T(8,128)(2,1)}, bf16[512,2048]{1,0:T(8,128)(2,1)}, s32[8,512]{1,0:T(8,128)}) custom-call(bf16[512,2048]{1,0:T(8,128)(2,1)} %x_ref.1, s32[2,512]{1,0:T(2,128)} %bitcast.9, bf16[2048,8,128]{2,1,0:T(8,128)(2,1)} %wq_ref.1, bf16[2048,128]{1,0:T(8,128)(2,1)} %bitcast.6, ...), custom_call_target="tpu_custom_call" | custom-call | tf_op jit(solution)/shard_map/front/pallas_call | solution.py:433
  206.4 103.7 %moe.1 = bf16[512,2048]{1,0:T(8,128)(2,1)} custom-call(bf16[16,128,2048]{2,1,0:T(8,128)(2,1)} %get-tuple-element.8.tok_ref, bf16[512,2048]{1,0:T(8,128)(2,1)} %get-tuple-element.9.h_ref, s32[8,512]{1,0:T(8,128)} %get-tuple-element.10.slot_ref, f32[2,512]{1,0:T(2,128)} %bitcast.8, bf16[16,2048,768]{2,1,0:T(8,128)(2,1)} %wg_ref.1, ...), custom_call_target="tpu_custom_call" | custom-call | tf_op jit(solution)/shard_map/moe/pallas_call | solution.py:452
  310.2 3.2 %copy.12 = bf16[512,2048]{1,0:T(8,128)(2,1)} copy(bf16[512,2048]{1,0:T(8,128)(2,1)} %moe.1) | data formatting | bytes 4194304
